TPU v7x, 128 devices: a whole 4x4x4 slice. The times are simulated.
128 devices in a mesh: rep: 16 (over z, x_lo, core), tp: 8 (over y, x_hi).
Axes of the slice: x: 4 (x_hi: 2, x_lo: 2; x = x_hi * 2 + x_lo), y: 4, z: 4, core: 2. Of those that a mesh axis runs over, the one named last changes fastest.
Arguments:
- hidden_state: bfloat16 [64, 3584], P('rep'), may hold values from -6 to 6
- lengths: int32 [64], P('rep'), may hold values from 1 to 4096, as said below
- old_qkv: bfloat16 [3584, 4608], P(None, 'tp'), may hold values from -0.09375 to 0.09375
- old_out: bfloat16 [3584, 3584], P(None, 'tp'), may hold values from -0.09375 to 0.09375
- cache_keys: bfloat16 [64, 4096, 512], P('rep', 'tp'), may hold values from -64 to 64
- cache_values: bfloat16 [64, 4096, 512], P('rep', 'tp'), may hold values from -6 to 6
- new_qkv: bfloat16 [3584, 4608], P(('rep', 'tp')), may hold values from -0.09375 to 0.09375
- new_out: bfloat16 [3584, 3584], P(('rep', 'tp')), may hold values from -0.09375 to 0.09375
Outputs:
- decoded: bfloat16 [64, 3584], P('rep', 'tp')
- resharded_qkv: bfloat16 [3584, 4608], P(None, 'tp')
- resharded_out: bfloat16 [3584, 3584], P(None, 'tp')
Inputs may be any that keep to these rules, and one draw needn't show every extreme that they name: Every sequence has 1 to 4096 cached tokens, held in positions 0 to lengths - 1; in every draw some sequence fills its cache.
All inputs are finite; a program needn't handle non-finite values.
Results may differ from a plain program's by a relative error of at most 0.012.
Values may be sent and summed in bfloat16 or wider, within the bound.
A program may use at most 128 MiB of HBM per device.

v0:
```python
import jax
import jax.numpy as jnp
from jax import lax
from jax.sharding import PartitionSpec as P

HQ = 28
KVH = 4
HD = 128


ROPE_BASE = 1000000.0


def in_order(tiles, dim):
    shape = list(tiles.shape[1:])
    shape[dim] *= tiles.shape[0]
    return jnp.moveaxis(tiles, 0, dim).reshape(shape)


def copy_for_each(x, axis):
    copies = jnp.broadcast_to(x, (lax.axis_size(axis), *x.shape))
    return lax.all_to_all(copies, axis, split_axis=0, concat_axis=0, tiled=True)


def gather_directly(x, axis, dim):
    return in_order(copy_for_each(x, axis), dim)


def taken_together(x, axis):
    return copy_for_each(x, axis).max(axis=0)


def taken_together_2(x, axis):
    everything = copy_for_each(x, axis)
    return jnp.sum(everything, axis=0)


def together(arrays, axis):
    ends = [0]
    for a in arrays:
        ends.append(ends[-1] + a.size)
    subtotal = taken_together_2(jnp.concatenate([a.ravel() for a in arrays]), axis)
    return tuple((subtotal[b:e].reshape(a.shape) for a, b, e in zip(arrays, ends, ends[1:])))


def rotate(vectors, positions):
    half_dim = vectors.shape[-1] // 2
    frequency = ROPE_BASE ** (-2.0 * jnp.arange(half_dim, dtype=jnp.float32) / (2 * half_dim))
    angles = positions.astype(jnp.float32)[:, None, None] * frequency
    first_half = vectors[..., :half_dim]
    second_half = vectors[..., half_dim:]
    return jnp.concatenate(
        [
            first_half * jnp.cos(angles) - second_half * jnp.sin(angles),
            second_half * jnp.cos(angles) + first_half * jnp.sin(angles),
        ],
        axis=-1,
    )


def per_device(hidden_state, lengths, old_qkv, old_out, cache_keys, cache_values, new_qkv, new_out):
    pieces = (
        lax.all_to_all(new_qkv, "tp", split_axis=1, concat_axis=0, tiled=True),
        lax.all_to_all(new_out, "tp", split_axis=1, concat_axis=0, tiled=True),
    )
    qkv_tp, out_tp = (
        lax.all_gather(pieces[0], "rep", axis=0, tiled=True),
        lax.all_gather(pieces[1], "rep", axis=0, tiled=True),
    )
    seq_count = hidden_state.shape[0]
    local_joined = jnp.dot(hidden_state, old_qkv, preferred_element_type=jnp.float32).astype(
        jnp.bfloat16
    )
    joined_rows = gather_directly(local_joined, "tp", 1)
    q_width = HQ * HD
    k_width = KVH * HD
    group_size = HQ // KVH
    queries = rotate(
        joined_rows[:, :q_width].astype(jnp.float32).reshape(seq_count, HQ, HD), lengths
    ).astype(jnp.bfloat16)
    own_keys = rotate(
        joined_rows[:, q_width : q_width + k_width].astype(jnp.float32).reshape(seq_count, KVH, HD),
        lengths,
    ).astype(jnp.bfloat16)
    own_values = joined_rows[:, q_width + k_width :].reshape(seq_count, KVH, HD)
    inv_root = 1.0 / jnp.sqrt(jnp.float32(HD))
    cache_rows = cache_keys.shape[1]
    grouped = queries.reshape(seq_count, KVH, group_size, HD)
    key_blocks = cache_keys.reshape(seq_count, cache_rows, KVH, HD)
    value_blocks = cache_values.reshape(seq_count, cache_rows, KVH, HD)
    scores = (
        jnp.einsum("skgd,stkd->skgt", grouped, key_blocks, preferred_element_type=jnp.float32)
        * inv_root
    )
    positions = lax.axis_index("tp") * cache_rows + jnp.arange(cache_rows, dtype=jnp.int32)
    live_mask = (positions[None, :] < lengths[:, None])[:, None, None, :]
    scores = jnp.where(live_mask, scores, jnp.float32(-1e30))
    own_score = (
        jnp.sum(grouped.astype(jnp.float32) * own_keys.astype(jnp.float32)[:, :, None, :], axis=-1)
        * inv_root
    )
    local_top = jnp.maximum(jnp.max(scores, axis=-1), own_score)
    top_score = taken_together(local_top, "tp")
    weights = jnp.where(live_mask, jnp.exp(scores - top_score[..., None]), jnp.float32(0.0)).astype(
        jnp.bfloat16
    )
    numer_part = jnp.einsum(
        "skgt,stkd->skgd", weights, value_blocks, preferred_element_type=jnp.float32
    )
    denom_part = jnp.sum(weights.astype(jnp.float32), axis=-1)
    numerator, denominator = together((numer_part, denom_part), "tp")
    own_weight = lax.optimization_barrier(
        jnp.exp(own_score - top_score).astype(jnp.bfloat16)
    ).astype(jnp.float32)
    numerator = numerator + own_weight[..., None] * own_values.astype(jnp.float32)[:, :, None, :]
    denominator = denominator + own_weight
    attended = (numerator / denominator[..., None]).reshape(seq_count, q_width).astype(jnp.bfloat16)
    decoded = jnp.dot(attended, old_out, preferred_element_type=jnp.float32).astype(jnp.bfloat16)
    return (decoded, qkv_tp, out_tp)


def solution(mesh):
    in_specs = (
        P("rep", None),
        P("rep"),
        P(None, "tp"),
        P(None, "tp"),
        P("rep", "tp", None),
        P("rep", "tp", None),
        P(("rep", "tp"), None),
        P(("rep", "tp"), None),
    )
    out_specs = (P("rep", "tp"), P(None, "tp"), P(None, "tp"))
    return jax.shard_map(
        per_device, mesh=mesh, in_specs=in_specs, out_specs=out_specs, check_vma=False
    )
```

profile of v0, /device:TPU:1, one launch (start us, length us, event | category | flops | bytes accessed | tf_op | source)
XLA Modules:
  0.0 118.5 jit_solution(7384145131231138753)
XLA Ops:
  7.2 0.0 copy-start
  7.2 0.0 all-gather.5.cloned.1.call-start
  7.2 1.4 %all_to_all.45 = bf16[28,8,448]{2,1,0:T(8,128)(2,1)S(1)} reshape(bf16[28,3584]{1,0:T(8,128)(2,1)} %param.15) | data formatting | bytes 401408 | tf_op jit(solution)/shard_map/all_to_all | solution.py:64
  8.6 0.1 copy.89
  8.7 14.9 %all_to_all.54 = bf16[28,8,448]{2,0,1:T(8,128)(2,1)S(1)} all-to-all(bf16[28,8,448]{2,0,1:T(8,128)(2,1)S(1)} %copy.89), channel_id=1, replica_groups=mesh['rep'=16,'tp'=8] {'tp'}, dimensions={1} | all-to-all | bytes 401408 | tf_op jit(solution)/shard_map/all_to_all | solution.py:64
  23.6 0.8 all_to_all.48
  24.4 0.0 all-gather.5.cloned.1.call-update
  24.4 0.0 all-gather.3.cloned.1.call-start
  24.4 1.2 %all_to_all.41 = bf16[28,8,576]{2,1,0:T(8,128)(2,1)S(1)} reshape(bf16[28,4608]{1,0:T(8,128)(2,1)} %param.14) | data formatting | bytes 516096 | tf_op jit(solution)/shard_map/all_to_all | solution.py:63
  25.7 10.6 %all_to_all.55 = bf16[28,8,576]{2,0,1:T(8,128)(2,1)S(1)} all-to-all(bf16[28,8,576]{2,0,1:T(8,128)(2,1)S(1)} %copy.88), channel_id=1, replica_groups=mesh['rep'=16,'tp'=8] {'tp'}, dimensions={1} | all-to-all | bytes 516096 | tf_op jit(solution)/shard_map/all_to_all | solution.py:63
  36.3 0.8 all_to_all.44
  37.1 0.0 all-gather.3.cloned.1.call-update
  37.1 0.0 copy-start.2
  37.1 3.4 %convolution_convert_fusion = bf16[4,576]{1,0:T(4,128)(2,1)S(1)} fusion(bf16[4,3584]{1,0:T(4,128)(2,1)} %param.8, bf16[3584,576]{0,1:T(8,128)(2,1)} %param.10), kind=kOutput, calls=%fused_computation.8 | convolution fusion | flops 16517376 | bytes 4162048 | tf_op jit(solution)/shard_map/dot_general | solution.py:71
  40.5 0.7 broadcast_in_dim.40
  41.2 3.3 %all-to-all-start = ((bf16[8,4,576]{2,1,0:T(4,128)(2,1)}), bf16[8,4,576]{2,1,0:T(4,128)(2,1)S(1)}, u32[]{:S(2)}, u32[]{:S(2)}) async-start(bf16[8,4,576]{2,1,0:T(4,128)(2,1)} %broadcast_in_dim.40), calls=%async_computation | async-start | bytes 81920 | tf_op jit(solution)/shard_map/all_to_all | solution.py:22
  44.5 0.0 copy-done.2
  44.6 0.1 multiply_cosine_fusion
  44.7 0.1 broadcast_compare_fusion
  44.8 6.3 %all-to-all-done = bf16[8,4,576]{2,1,0:T(4,128)(2,1)S(1)} async-done(((bf16[8,4,576]{2,1,0:T(4,128)(2,1)}), bf16[8,4,576]{2,1,0:T(4,128)(2,1)S(1)}, u32[]{:S(2)}, u32[]{:S(2)}) %all-to-all-start) | async-done | bytes 36896 | tf_op jit(solution)/shard_map/all_to_all | solution.py:22
  51.1 0.1 reshape.181
  51.3 0.1 subtract_convert_fusion
  51.5 0.1 subtract_convert_fusion.1
  51.6 0.1 maximum_convert_fusion
  51.6 0.2 multiply_reduce_fusion
  51.8 2.4 %fusion.16 = (f32[4,4,7]{2,1,0:T(4,128)S(1)}, f32[4,4,7,512]{3,2,1,0:T(8,128)S(1)}) fusion(bf16[4,4,7,64]{3,2,1,0:T(8,128)(2,1)S(1)} %copy.81, bf16[4,4,7,64]{3,2,1,0:T(8,128)(2,1)S(1)} %copy.80, pred[4,512]{1,0:T(4,128)(4,1)S(1)} %broadcast_compare_fusion, bf16[4,512,512]{2,1,0:T(8,128)(2,1)} %param.12), kind=kOutput, calls=%fused_computation.36 | convolution fusion | flops 14909328 | bytes 2357696 | tf_op jit(solution)/shard_map/skgd,stkd->skgt/dot_general | solution.py:92
  54.2 0.0 copy-done.1
  54.3 0.6 broadcast_in_dim.42
  54.9 3.4 %all-to-all-start.1 = ((f32[8,4,4,7]{3,2,1,0:T(4,128)}), f32[8,4,4,7]{3,2,1,0:T(4,128)S(1)}, u32[]{:S(2)}, u32[]{:S(2)}) async-start(f32[8,4,4,7]{3,2,1,0:T(4,128)} %broadcast_in_dim.42), calls=%async_computation.1 | async-start | bytes 131072 | tf_op jit(solution)/shard_map/all_to_all | solution.py:22
  58.3 0.6 reshape.196
  58.9 6.0 %all-to-all-done.1 = f32[8,4,4,7]{3,2,1,0:T(4,128)S(1)} async-done(((f32[8,4,4,7]{3,2,1,0:T(4,128)}), f32[8,4,4,7]{3,2,1,0:T(4,128)S(1)}, u32[]{:S(2)}, u32[]{:S(2)}) %all-to-all-start.1) | async-done | bytes 3616 | tf_op jit(solution)/shard_map/all_to_all | solution.py:22
  64.9 2.0 %fusion = f32[4,4,7,128]{3,2,1,0:T(8,128)S(1)} fusion(f32[4,4,7,512]{3,2,1,0:T(8,128)S(1)} %get-tuple-element.30, f32[4,4,7]{2,1,0:T(4,128)S(1)} %reduce_max.19, pred[4,512]{1,0:T(4,128)(4,1)} %copy-done.1, bf16[4,512,512]{2,1,0:T(8,128)(2,1)} %param.13), kind=kOutput, calls=%fused_computation | convolution fusion | flops 14852096 | bytes 2386368 | tf_op jit(solution)/shard_map/skgt,stkd->skgd/dot_general | solution.py:107
  67.0 0.6 reshape.188
  67.6 0.9 convert_reduce_fusion
  68.5 0.1 reshape.189
  68.6 0.8 pad_maximum_fusion
  69.4 1.0 broadcast_in_dim.44
  70.4 4.2 %all-to-all-start.2 = ((f32[8,1,14448]{2,1,0:T(1,128)}), f32[8,1,14448]{2,1,0:T(1,128)}, u32[]{:S(2)}, u32[]{:S(2)}) async-start(f32[8,1,14448]{2,1,0:T(1,128)} %broadcast_in_dim.44), calls=%async_computation.2 | async-start | bytes 925696 | tf_op jit(solution)/shard_map/all_to_all | solution.py:22
  74.6 0.8 broadcast_multiply_fusion
  75.4 12.6 %all-to-all-done.2 = f32[8,1,14448]{2,1,0:T(1,128)} async-done(((f32[8,1,14448]{2,1,0:T(1,128)}), f32[8,1,14448]{2,1,0:T(1,128)}, u32[]{:S(2)}, u32[]{:S(2)}) %all-to-all-start.2) | async-done | bytes 462368 | tf_op jit(solution)/shard_map/all_to_all | solution.py:22
  88.0 1.4 %reduce_sum.29 = f32[14448]{0:T(1024)S(1)} reduce(f32[8,1,14448]{2,1,0:T(1,128)} %all-to-all-done.2, f32[]{:T(128)} %constant.7.clone.1), dimensions={0,1}, to_apply=%region_4.5 | reduce | flops 101136 | bytes 520132 | tf_op jit(solution)/shard_map/reduce_sum | solution.py:35
  89.4 0.1 reshape.191
  89.5 0.1 div.19
  89.7 0.0 copy-done
  89.7 1.6 %convolution_convert_fusion.1 = bf16[4,448]{1,0:T(4,128)(2,1)} fusion(bf16[3584,448]{0,1:T(8,128)(2,1)S(1)} %copy-done, f32[4,3584]{1,0:T(4,128)S(1)} %div.20, f32[4,3584]{1,0:T(4,128)S(1)} %reshape.190, f32[4,3584]{1,0:T(4,128)S(1)} %mul.152), kind=kOutput, calls=%fused_computation.9 | convolution fusion | flops 12889856 | bytes 3386880 | tf_op jit(solution)/shard_map/dot_general | solution.py:118
  91.2 5.7 %copy.91 = bf16[3584,448]{0,1:T(8,128)(2,1)} copy(bf16[3584,448]{1,0:T(8,128)(2,1)} %all-gather.5.cloned.1.call-done) | data formatting | bytes 6422528
  96.9 8.3 %all-gather.3.cloned.1.call-done = bf16[3584,576]{1,0:T(8,128)(2,1)} async-done(((bf16[224,576]{1,0:T(8,128)(2,1)}), bf16[3584,576]{1,0:T(8,128)(2,1)}) %all-gather.3.cloned.1.call-update) | async-done | bytes 4128784 | tf_op jit(solution)/shard_map/all_gather | solution.py:67
  105.2 6.5 %copy.90 = bf16[3584,576]{0,1:T(8,128)(2,1)} copy(bf16[3584,576]{1,0:T(8,128)(2,1)} %all-gather.3.cloned.1.call-done) | data formatting | bytes 8257536
  (25 shorter events, 0.4 us)
Async XLA Ops:
  7.2 82.5 %copy-start = (bf16[3584,448]{0,1:T(8,128)(2,1)S(1)}, bf16[3584,448]{0,1:T(8,128)(2,1)}, u32[]{:S(2)}) copy-start(bf16[3584,448]{0,1:T(8,128)(2,1)} %param.11) | copy-start | bytes 9633796
  7.2 84.1 %all-gather.5.cloned.1.call-start = ((), (), s32[]{:S(2)}) async-start(), calls=%async_computation.6 | async-start | bytes 3899392 | tf_op jit(solution)/shard_map/all_gather | solution.py:68
  24.4 80.8 %all-gather.3.cloned.1.call-start = ((), (), s32[]{:S(2)}) async-start(), calls=%async_computation.5 | async-start | bytes 4874240 | tf_op jit(solution)/shard_map/all_gather | solution.py:67
  37.1 7.5 %copy-start.2 = (s32[4]{0:T(128)S(1)}, s32[4]{0:T(128)}, u32[]{:S(2)}) copy-start(s32[4]{0:T(128)} %param.9) | copy-start | bytes 52
  41.2 9.9 %all-to-all-start = ((bf16[8,4,576]{2,1,0:T(4,128)(2,1)}), bf16[8,4,576]{2,1,0:T(4,128)(2,1)S(1)}, u32[]{:S(2)}, u32[]{:S(2)}) async-start(bf16[8,4,576]{2,1,0:T(4,128)(2,1)} %broadcast_in_dim.40), calls=%async_computation | async-start | bytes 81920 | tf_op jit(solution)/shard_map/all_to_all | solution.py:22
  44.8 9.4 %copy-start.1 = (pred[4,512]{1,0:T(4,128)(4,1)}, pred[4,512]{1,0:T(4,128)(4,1)S(1)}, u32[]{:S(2)}) copy-start(pred[4,512]{1,0:T(4,128)(4,1)S(1)} %broadcast_compare_fusion) | copy-start | bytes 6148
  54.9 10.0 %all-to-all-start.1 = ((f32[8,4,4,7]{3,2,1,0:T(4,128)}), f32[8,4,4,7]{3,2,1,0:T(4,128)S(1)}, u32[]{:S(2)}, u32[]{:S(2)}) async-start(f32[8,4,4,7]{3,2,1,0:T(4,128)} %broadcast_in_dim.42), calls=%async_computation.1 | async-start | bytes 131072 | tf_op jit(solution)/shard_map/all_to_all | solution.py:22
  70.4 17.6 %all-to-all-start.2 = ((f32[8,1,14448]{2,1,0:T(1,128)}), f32[8,1,14448]{2,1,0:T(1,128)}, u32[]{:S(2)}, u32[]{:S(2)}) async-start(f32[8,1,14448]{2,1,0:T(1,128)} %broadcast_in_dim.44), calls=%async_computation.2 | async-start | bytes 925696 | tf_op jit(solution)/shard_map/all_to_all | solution.py:22
Sparse Core Ops, SparseCore 0:
  24.5 36.5 all-gather.4
  63.4 41.7 all-gather.2
where the time goes:
time: 119 us
  waiting for transfers between devices  33.3 us (28%)
  blocking collectives  25.5 us (21%)
  local copies, waits for them, and re-layouts  20.6 us (17%)
  between operations  14.3 us (12%)
  starting transfers between devices  10.9 us (9%)
  matrix products  9.43 us (8%)
  other arithmetic  4.59 us (4%)
    all_to_all x3, waiting for transfers between devices, copy_for_each(): return lax.all_to_all(copies, axis, split_axis=0, concat_axis=0, tiled=True)  24.9 us
    all_to_all x1, blocking collectives, per_device(): lax.all_to_all(new_out, 'tp', split_axis=1, concat_axis=0, tiled=True)  14.9 us
    unnamed x8, local copies, waits for them, and re-layouts  12.2 us
    all_to_all x3, starting transfers between devices, copy_for_each(): return lax.all_to_all(copies, axis, split_axis=0, concat_axis=0, tiled=True)  10.8 us
    all_to_all x1, blocking collectives, per_device(): lax.all_to_all(new_qkv, 'tp', split_axis=1, concat_axis=0, tiled=True)  10.6 us
    all_gather x1, waiting for transfers between devices, per_device(): lax.all_gather(pieces[0], 'rep', axis=0, tiled=True)  8.3 us
    dot_general x1, matrix products, per_device(): jnp.dot(hidden_state, old_qkv, preferred_element_type=jnp.float32)  3.43 us
    dot_general x1, matrix products, per_device(): jnp.einsum('skgd,stkd->skgt', grouped, key_blocks, preferred_element_type...  2.4 us
  transfers between devices with their start and end apart: 5, of which 4 were waited for; matrix products, arithmetic and copies ran while one was open for 20% of the time, Pallas kernels for 0%

commit v1 on v0

v1 whole, which is shorter than its diff:
```python
import functools

import jax
import jax.numpy as jnp
from jax import lax
from jax.experimental import pallas as pl
from jax.experimental.pallas import tpu as pltpu
from jax.sharding import PartitionSpec as P

HQ = 28
KVH = 4
HD = 128
GROUP = HQ // KVH
ROPE_BASE = 1000000.0
ROWS = 28
QC = 576
OC = 448
TILES = 8
SLOT = ROWS * TILES
SEQ = 4
CHUNK = 512
PAIRS = SEQ * KVH

ITEMS = ((0, 0), (0, 1), (1, 0), (3, 0), (1, 1), (3, 1), (2, 0), (2, 1))
X_FIRST = (True, True, False, True, False, True, False, True)
F32 = jnp.float32
BF16 = jnp.bfloat16


def move_kernel(
    len_smem, hidden, trig, old_qkv, old_out, keys, values, new_qkv, new_out,
    land, decoded,
    packed, nq, no, hid, trg, wq, wo, kb, vb,
    jown, jall, jfull, qf, ownb, part, parts, att, amat, lensem,
    load_sem, recv_sem, send_sem, small_recv, small_send,
):
    rep = lax.axis_index("rep")
    tp = lax.axis_index("tp")
    core = rep % 2
    x_lo = (rep // 2) % 2
    z = rep // 4
    y = tp // 2
    x_hi = tp % 2
    z_up = (z + 1) % 4
    z_dn = (z + 3) % 4
    z_op = (z + 2) % 4
    x_ot = 1 - x_lo

    def rep_of(zz, xx, cc):
        return (zz * 2 + xx) * 2 + cc

    loads = []
    for n, (src, dst) in enumerate(
        ((new_qkv, nq), (new_out, no), (hidden, hid), (trig, trg), (old_qkv, wq), (keys, kb), (values, vb), (old_out, wo))
    ):
        c = pltpu.make_async_copy(src, dst, load_sem.at[n])
        c.start()
        loads.append(c)

    barrier = pltpu.get_barrier_semaphore()
    friends = []
    for dy in range(4):
        for f in range(2):
            t = ((y + dy) % 4) * 2 + (x_hi + f) % 2
            if (dy, f) != (0, 0):
                friends.append((rep, t))
            if f == 1:
                friends.append((rep_of(z, x_ot, core), t))
    friends.append((rep_of(z, x_ot, core), tp))
    friends.append((rep_of(z_up, x_lo, core), tp))
    friends.append((rep_of(z_dn, x_lo, core), tp))
    friends.append((rep_of(z, x_lo, 1 - core), tp))
    for r, t in friends:
        pl.semaphore_signal(barrier, inc=1, device_id={"rep": r, "tp": t}, device_id_type=pl.DeviceIdType.MESH)

    loads[0].wait()
    loads[1].wait()
    for t in range(8):
        a = nq[:, QC * t : QC * (t + 1)]
        b = no[:, OC * t : OC * (t + 1)]
        for k in range(TILES):
            if k < 4:
                v = a[:, 128 * k : 128 * (k + 1)]
            elif k == 4:
                v = jnp.concatenate([a[:, 512:576], b[:, 384:448]], axis=1)
            else:
                v = b[:, 128 * (k - 5) : 128 * (k - 4)]
            packed[t, ROWS * k : ROWS * (k + 1), :] = v
    mine = rep * 8 + tp
    land[mine] = packed[tp]
    pl.semaphore_wait(barrier, len(friends))

    sent = []

    def put(src, slot, r, t):
        c = pltpu.make_async_remote_copy(
            src_ref=src, dst_ref=land.at[slot], send_sem=send_sem.at[len(sent)], recv_sem=recv_sem.at[slot],
            device_id={"rep": r, "tp": t}, device_id_type=pl.DeviceIdType.MESH,
        )
        c.start()
        sent.append(c)

    def arrived(slot):
        pltpu.make_async_remote_copy(
            src_ref=land.at[slot], dst_ref=land.at[slot], send_sem=send_sem.at[0], recv_sem=recv_sem.at[slot],
            device_id={"rep": rep, "tp": tp}, device_id_type=pl.DeviceIdType.MESH,
        ).wait_recv()

    def slot_of(zz, xx, item):
        dy, f = item
        r = rep_of(zz, (xx + f) % 2, core)
        t = ((y + dy) % 4) * 2 + (x_hi + f) % 2
        return r * 8 + t

    def exchange():
        for dy, f in ITEMS[1:]:
            t = ((y + 4 - dy) % 4) * 2 + (x_hi + f) % 2
            put(packed.at[t], mine, rep_of(z, (x_lo + f) % 2, core), t)

    def up(slot):
        put(land.at[slot], slot, rep_of(z_up, x_lo, core), tp)

    def down(slot):
        put(land.at[slot], slot, rep_of(z_dn, x_lo, core), tp)

    def across(slot):
        put(land.at[slot], slot, rep_of(z, x_ot, core), tp)

    def twin(slot):
        put(land.at[slot], slot, rep_of(z, x_lo, 1 - core), tp)

    def step(s):
        if 0 <= s < 8:
            b = slot_of(z, x_lo, ITEMS[s])
            if s:
                arrived(b)
            across(b)
            up(b)
            down(b)
            twin(b)
        j = s - 1
        if 0 <= j < 8:
            it = ITEMS[j]
            b = slot_of(z, x_ot, it)
            arrived(b)
            if X_FIRST[j]:
                up(b)
                down(b)
            twin(b)
            for zz, go, fwd in ((z_dn, up, j % 2 == 0), (z_up, down, j % 2 == 1)):
                b = slot_of(zz, x_lo, it)
                arrived(b)
                if fwd:
                    go(b)
                if not X_FIRST[j]:
                    across(b)
                twin(b)
        j = s - 2
        if 0 <= j < 8:
            it = ITEMS[j]
            for zz, go, fwd in ((z_dn, up, j % 2 == 1), (z_up, down, j % 2 == 0)):
                b = slot_of(zz, x_ot, it)
                arrived(b)
                if fwd and X_FIRST[j]:
                    go(b)
                twin(b)
            b = slot_of(z_op, x_lo, it)
            arrived(b)
            if not X_FIRST[j]:
                across(b)
            twin(b)
        j = s - 3
        if 0 <= j < 8:
            b = slot_of(z_op, x_ot, ITEMS[j])
            arrived(b)
            twin(b)

    small = []

    def to_peers(phase, src_of, dst_of):
        for n in range(1, 8):
            t = (tp + n) % 8
            c = pltpu.make_async_remote_copy(
                src_ref=src_of(t), dst_ref=dst_of(), send_sem=small_send.at[phase, n - 1],
                recv_sem=small_recv.at[phase, tp],
                device_id={"rep": rep, "tp": t}, device_id_type=pl.DeviceIdType.MESH,
            )
            c.start()
            small.append(c)

    def from_peers(phase, dst_from):
        for n in range(1, 8):
            t = (tp + 8 - n) % 8
            pltpu.make_async_remote_copy(
                src_ref=dst_from(t), dst_ref=dst_from(t), send_sem=small_send.at[phase, 0],
                recv_sem=small_recv.at[phase, t],
                device_id={"rep": rep, "tp": tp}, device_id_type=pl.DeviceIdType.MESH,
            ).wait_recv()

    def project():
        loads[2].wait()
        loads[4].wait()
        res = jnp.dot(hid[...], wq[...], preferred_element_type=F32).astype(BF16)
        jown[0:SEQ, 0:QC] = res
        jall[tp, 0:SEQ, 0:QC] = res
        to_peers(0, lambda t: jown, lambda: jall.at[tp])

    def rotary():
        from_peers(0, lambda t: jall.at[t])
        loads[3].wait()
        for t in range(8):
            jfull[0:SEQ, QC * t : QC * (t + 1)] = jall[t, 0:SEQ, 0:QC].astype(F32)
        cos2 = trg[0:SEQ, :]
        sin2 = trg[8 : 8 + SEQ, :]
        for h in range(HQ + KVH):
            x = jfull[0:SEQ, HD * h : HD * (h + 1)]
            r = x * cos2 + pltpu.roll(x, HD // 2, 1) * sin2
            qf[8 * h : 8 * h + SEQ, :] = r.astype(BF16).astype(F32)
        inv_root = 1.0 / jnp.sqrt(F32(HD))
        for s in range(SEQ):
            for k in range(KVH):
                q = qf[pl.ds(8 * GROUP * k + s, 8, stride=8), :]
                key = qf[8 * (HQ + k) + s : 8 * (HQ + k) + s + 1, :]
                own = jnp.sum(q * key, axis=1, keepdims=True) * inv_root
                ownb[s * KVH + k, 0:8, :] = jnp.broadcast_to(own, (8, HD))
                c0 = HQ * HD + KVH * HD + HD * k
                ownb[s * KVH + k, 8:16, :] = jnp.broadcast_to(jfull[s : s + 1, c0 : c0 + HD], (8, HD))

    def attend(s):
        if s == 0:
            loads[5].wait()
            loads[6].wait()
        inv_root = 1.0 / jnp.sqrt(F32(HD))
        pos = lax.broadcasted_iota(jnp.int32, (8, CHUNK), 1) + tp * CHUNK
        live = pos < len_smem[s]
        lane = lax.broadcasted_iota(jnp.int32, (8, HD), 1)
        for k in range(KVH):
            q = qf[pl.ds(8 * GROUP * k + s, 8, stride=8), :].astype(BF16)
            sc = lax.dot_general(
                q, kb[s, :, HD * k : HD * (k + 1)], (((1,), (1,)), ((), ())), preferred_element_type=F32
            ) * inv_root
            sc = jnp.where(live, sc, F32(-1e30))
            m = jnp.max(sc, axis=1, keepdims=True)
            p = jnp.where(live, jnp.exp(sc - m), F32(0.0)).astype(BF16)
            l = jnp.sum(p.astype(F32), axis=1, keepdims=True)
            n = jnp.dot(p, vb[s, :, HD * k : HD * (k + 1)], preferred_element_type=F32)
            part[s * KVH + k, 0:8, :] = n
            part[s * KVH + k, 8:16, :] = jnp.where(
                lane == 0, jnp.broadcast_to(m, (8, HD)), jnp.broadcast_to(l, (8, HD))
            )

    def share():
        parts[tp] = part[pl.ds(2 * tp, 2)]
        to_peers(1, lambda t: part.at[pl.ds(2 * t, 2)], lambda: parts.at[tp])

    def combine():
        from_peers(1, lambda t: parts.at[t])
        for n in range(2):
            own = ownb[2 * tp + n, 0:8, :]
            val = ownb[2 * tp + n, 8:16, :]
            top = own
            for t in range(8):
                top = jnp.maximum(top, jnp.broadcast_to(parts[t, n, 8:16, 0:1], (8, HD)))
            w = jnp.exp(own - top).astype(BF16).astype(F32)
            num = w * val
            den = w
            for t in range(8):
                scale = jnp.exp(jnp.broadcast_to(parts[t, n, 8:16, 0:1], (8, HD)) - top)
                num = num + parts[t, n, 0:8, :] * scale
                den = den + jnp.broadcast_to(parts[t, n, 8:16, 1:2], (8, HD)) * scale
            att[2 * tp + n] = (num / den).astype(BF16).astype(F32)
        to_peers(2, lambda t: att.at[pl.ds(2 * tp, 2)], lambda: att.at[pl.ds(2 * tp, 2)])

    def finish():
        from_peers(2, lambda t: att.at[pl.ds(2 * t, 2)])
        loads[7].wait()
        for k in range(KVH):
            for g in range(GROUP):
                h = GROUP * k + g
                for s in range(SEQ):
                    amat[s : s + 1, HD * h : HD * (h + 1)] = att[s * KVH + k, g : g + 1, :]
        decoded[...] = jnp.dot(
            amat[0:SEQ, :].astype(BF16), wo[...], preferred_element_type=F32
        ).astype(BF16)

    step(0)
    exchange()
    project()
    step(1)
    step(2)
    rotary()
    step(3)
    attend(0)
    attend(1)
    step(4)
    attend(2)
    attend(3)
    share()
    step(5)
    step(6)
    combine()
    step(7)
    step(8)
    finish()
    step(9)
    step(10)
    for it in ITEMS:
        for zz in (z, z_dn, z_up, z_op):
            for xx in (x_lo, x_ot):
                b = slot_of(zz, xx, it)
                arrived(b + 8 * (1 - 2 * core))
    for c in sent:
        c.wait_send()
    for c in small:
        c.wait_send()


def write_kernel(land, dec, out_q, out_o, out_d, oq, oo, sems):
    parts = 8
    rows = 3584 // parts
    copies = []
    d = pltpu.make_async_copy(dec, out_d, sems.at[2 * parts])
    d.start()
    for p in range(parts):

        def body(i, _):
            r0 = pl.multiple_of(p * rows + i * 112, 112)
            tq = oq.at[pl.ds(r0, 112)]
            to = oo.at[pl.ds(r0, 112)]
            for m in range(4):
                b = p * 16 + i * 4 + m
                for k in range(TILES):
                    v = land[b, ROWS * k : ROWS * (k + 1), :]
                    at = pl.ds(ROWS * m, ROWS)
                    if k < 4:
                        tq[at, 128 * k : 128 * (k + 1)] = v
                    elif k == 4:
                        tq[at, 512:576] = v[:, 0:64]
                        to[at, 384:448] = v[:, 64:128]
                    else:
                        to[at, 128 * (k - 5) : 128 * (k - 4)] = v
            return 0

        lax.fori_loop(0, rows // 112, body, 0)
        for n, (src, dst) in enumerate(((oq, out_q), (oo, out_o))):
            c = pltpu.make_async_copy(src.at[pl.ds(p * rows, rows)], dst.at[pl.ds(p * rows, rows)], sems.at[2 * p + n])
            c.start()
            copies.append(c)
    for c in copies:
        c.wait()
    d.wait()


def per_device(hidden_state, lengths, old_qkv, old_out, cache_keys, cache_values, new_qkv, new_out):
    half = HD // 2
    frequency = ROPE_BASE ** (-2.0 * jnp.arange(half, dtype=F32) / (2 * half))
    angles = lengths.astype(F32)[:, None] * frequency
    cos, sin = jnp.cos(angles), jnp.sin(angles)
    pad = jnp.zeros((4, HD), F32)
    trig = jnp.concatenate(
        [jnp.concatenate([cos, cos], 1), pad, jnp.concatenate([-sin, sin], 1), pad], 0
    )
    any_ = pl.BlockSpec(memory_space=pl.ANY)
    vmem = pl.BlockSpec(memory_space=pltpu.VMEM)
    land, dec = pl.pallas_call(
        move_kernel,
        out_shape=(pltpu.VMEM((128, SLOT, 128), BF16), pltpu.VMEM((SEQ, OC), BF16)),
        in_specs=[pl.BlockSpec(memory_space=pltpu.SMEM)] + [any_] * 8,
        out_specs=(vmem, vmem),
        scratch_shapes=[
            pltpu.VMEM((8, SLOT, 128), BF16),
            pltpu.VMEM((ROWS, 4608), BF16),
            pltpu.VMEM((ROWS, 3584), BF16),
            pltpu.VMEM((SEQ, 3584), BF16),
            pltpu.VMEM((16, HD), F32),
            pltpu.VMEM((3584, QC), BF16),
            pltpu.VMEM((3584, OC), BF16),
            pltpu.VMEM((SEQ, CHUNK, 512), BF16),
            pltpu.VMEM((SEQ, CHUNK, 512), BF16),
            pltpu.VMEM((16, 640), BF16),
            pltpu.VMEM((8, 16, 640), BF16),
            pltpu.VMEM((8, 4608), F32),
            pltpu.VMEM((8 * (HQ + KVH), HD), F32),
            pltpu.VMEM((PAIRS, 16, HD), F32),
            pltpu.VMEM((PAIRS, 16, HD), F32),
            pltpu.VMEM((8, 2, 16, HD), F32),
            pltpu.VMEM((PAIRS, 8, HD), F32),
            pltpu.VMEM((8, 3584), F32),
            pltpu.SemaphoreType.REGULAR,
            pltpu.SemaphoreType.DMA((8,)),
            pltpu.SemaphoreType.DMA((128,)),
            pltpu.SemaphoreType.DMA((128,)),
            pltpu.SemaphoreType.DMA((3, 8)),
            pltpu.SemaphoreType.DMA((3, 7)),
        ],
        compiler_params=pltpu.CompilerParams(
            collective_id=0, has_side_effects=True, vmem_limit_bytes=40 * 1024 * 1024
        ),
        name="move",
    )(lengths, hidden_state, trig, old_qkv, old_out, cache_keys, cache_values, new_qkv, new_out)
    qkv_tp, out_tp, decoded = pl.pallas_call(
        write_kernel,
        out_shape=(
            jax.ShapeDtypeStruct((3584, QC), BF16),
            jax.ShapeDtypeStruct((3584, OC), BF16),
            jax.ShapeDtypeStruct((SEQ, OC), BF16),
        ),
        in_specs=[vmem, vmem],
        out_specs=(any_, any_, any_),
        scratch_shapes=[
            pltpu.VMEM((3584, QC), BF16),
            pltpu.VMEM((3584, OC), BF16),
            pltpu.SemaphoreType.DMA((17,)),
        ],
        compiler_params=pltpu.CompilerParams(vmem_limit_bytes=24 * 1024 * 1024),
        name="write",
    )(land, dec)
    return decoded, qkv_tp, out_tp


def solution(mesh):
    in_specs = (
        P("rep", None),
        P("rep"),
        P(None, "tp"),
        P(None, "tp"),
        P("rep", "tp", None),
        P("rep", "tp", None),
        P(("rep", "tp"), None),
        P(("rep", "tp"), None),
    )
    out_specs = (P("rep", "tp"), P(None, "tp"), P(None, "tp"))
    return jax.shard_map(per_device, mesh=mesh, in_specs=in_specs, out_specs=out_specs, check_vma=False)
```

time: 119 us -> 90.8 us (0.76)
  Pallas kernels: 0 us -> 58.6 us
  waiting for transfers between devices: 33.3 us -> 0 us
  blocking collectives: 25.5 us -> 0 us
  between operations: 14.3 us -> 0.71 us
  starting transfers between devices: 10.9 us -> 0 us
  local copies, waits for them, and re-layouts: 20.6 us -> 30.1 us
  matrix products: 9.43 us -> 0 us
  other arithmetic: 4.59 us -> 0.86 us
    pallas_call x0 -> x2, Pallas kernels: none -> 58.6 us  [the longest x1 51.9 us: per_device(): pl.pallas_call(move_kernel, out_shape=(pltpu.VMEM((128, SLOT, 128), BF16)...]
    all_to_all x2 -> x0, blocking collectives: 25.5 us -> none  [the longest x1 14.9 us: per_device(): lax.all_to_all(new_out, 'tp', split_axis=1, concat_axis=0, tiled=True)]
    all_to_all x3 -> x0, waiting for transfers between devices: 24.9 us -> none  [copy_for_each(): return lax.all_to_all(copies, axis, split_axis=0, concat_axis=0, tiled=True)]
    unnamed x8 -> x20, local copies, waits for them, and re-layouts: 12.2 us -> 30.1 us
    all_to_all x3 -> x0, starting transfers between devices: 10.8 us -> none  [copy_for_each(): return lax.all_to_all(copies, axis, split_axis=0, concat_axis=0, tiled=True)]
    dot_general x4 -> x0, matrix products: 9.43 us -> none  [the longest x1 3.43 us: per_device(): jnp.dot(hidden_state, old_qkv, preferred_element_type=jnp.float32)]
    all_gather x2 -> x0, waiting for transfers between devices: 8.31 us -> none  [the longest x1 8.3 us: per_device(): lax.all_gather(pieces[0], 'rep', axis=0, tiled=True)]
    all_to_all x6 -> x0, local copies, waits for them, and re-layouts: 4.27 us -> none  [the longest x3 2.22 us: per_device(): lax.all_to_all(new_out, 'tp', split_axis=1, concat_axis=0, tiled=True)]
  transfers between devices with their start and end apart: 5 -> 0, of which waited for: 4 -> 0; matrix products, arithmetic and copies ran while one was open for 20% -> 0% of each run, Pallas kernels for 0% -> 0%
where the time goes in v1:
time: 90.8 us; the launch traced here: 90.2 us
  Pallas kernels  58.6 us (65%)
  local copies, waits for them, and re-layouts  30.1 us (33%)
    pallas_call x1, Pallas kernels, per_device(): pl.pallas_call(move_kernel, out_shape=(pltpu.VMEM((128, SLOT, 128), BF16)...  51.9 us
    unnamed x20, local copies, waits for them, and re-layouts  30.1 us
    pallas_call x1, Pallas kernels, per_device(): pl.pallas_call(write_kernel, out_shape=(jax.ShapeDtypeStruct((3584, QC),...  6.72 us

profile of v1, /device:TPU:1, one launch (start us, length us, event | category | flops | bytes accessed | tf_op | source)
XLA Modules:
  0.0 90.2 jit_solution(1661552307900862338)
XLA Ops:
  0.6 0.7 convert_element_type.3
  1.3 0.1 multiply_cosine_fusion
  1.4 0.1 pad_maximum_fusion.trig
  1.5 5.7 %copy.12.old_out = bf16[3584,448]{1,0:T(8,128)(2,1)} copy(bf16[3584,448]{0,1:T(8,128)(2,1)} %param.11) | data formatting | bytes 6422528 | tf_op args[3]
  7.2 0.0 copy-start.2
  7.2 0.0 copy-start.4
  7.3 0.0 copy-start.5
  7.3 0.0 copy-start.6
  7.3 0.0 copy-start.7
  7.3 6.7 %copy.11.old_qkv = bf16[3584,576]{1,0:T(8,128)(2,1)} copy(bf16[3584,576]{0,1:T(8,128)(2,1)} %param.10) | data formatting | bytes 8257536 | tf_op args[2]
  13.9 0.0 copy-done.2
  13.9 0.0 copy-done.4
  13.9 0.0 copy-done.5
  13.9 0.0 copy-done.6
  14.0 0.0 copy-done.7
  14.0 0.0 copy-start.3
  14.0 1.6 %copy-done.3 = bf16[4,512,512]{2,1,0:T(8,128)(2,1)S(1)} copy-done((bf16[4,512,512]{2,1,0:T(8,128)(2,1)S(1)}, bf16[4,512,512]{2,1,0:T(8,128)(2,1)}, u32[]{:S(2)}) %copy-start.3) | copy-done | bytes 2097176
  15.6 51.9 %move.1 = (bf16[128,224,128]{2,1,0:T(8,128)(2,1)S(1)}, bf16[4,448]{1,0:T(4,128)(2,1)S(1)}) custom-call(s32[4]{0:T(128)S(1)} %copy-done.7, bf16[4,3584]{1,0:T(4,128)(2,1)S(1)} %copy-done.6, f32[16,128]{1,0:T(8,128)S(1)} %pad_maximum_fusion.trig, bf16[3584,576]{1,0:T(8,128)(2,1)} %copy.11.old_qkv, bf16[3584,448]{1,0:T(8,128)(2,1)} %copy.12.old_out, ...), custom_call_target="tpu_custom_call" | custom-call | tf_op jit(solution)/shard_map/move/pallas_call | solution.py:365
  67.4 6.7 %write.1 = (bf16[3584,576]{1,0:T(8,128)(2,1)S(1)}, bf16[3584,448]{1,0:T(8,128)(2,1)S(1)}, bf16[4,448]{1,0:T(4,128)(2,1)}) custom-call(bf16[128,224,128]{2,1,0:T(8,128)(2,1)S(1)} %get-tuple-element.8.land, bf16[4,448]{1,0:T(4,128)(2,1)S(1)} %get-tuple-element.9.dec), custom_call_target="tpu_custom_call" | custom-call | tf_op jit(solution)/shard_map/write/pallas_call | solution.py:401
  74.2 0.0 copy-start
  74.2 2.1 %copy-done = bf16[3584,576]{1,0:T(8,128)(2,1)} copy-done((bf16[3584,576]{1,0:T(8,128)(2,1)}, bf16[3584,576]{1,0:T(8,128)(2,1)S(1)}, u32[]{:S(2)}) %copy-start) | copy-done | bytes 4128792
  76.2 0.0 copy-start.1
  76.3 1.8 %copy-done.1 = bf16[3584,448]{1,0:T(8,128)(2,1)} copy-done((bf16[3584,448]{1,0:T(8,128)(2,1)}, bf16[3584,448]{1,0:T(8,128)(2,1)S(1)}, u32[]{:S(2)}) %copy-start.1) | copy-done | bytes 3211288
  78.1 5.7 %copy.14 = bf16[3584,448]{0,1:T(8,128)(2,1)} copy(bf16[3584,448]{1,0:T(8,128)(2,1)} %copy-done.1) | data formatting | bytes 6422528
  83.8 6.5 %copy.13 = bf16[3584,576]{0,1:T(8,128)(2,1)} copy(bf16[3584,576]{1,0:T(8,128)(2,1)} %copy-done) | data formatting | bytes 8257536
  (2 shorter events, 0.0 us)
Async XLA Ops:
  7.2 6.7 %copy-start.2 = (bf16[4,512,512]{2,1,0:T(8,128)(2,1)S(1)}, bf16[4,512,512]{2,1,0:T(8,128)(2,1)}, u32[]{:S(2)}) copy-start(bf16[4,512,512]{2,1,0:T(8,128)(2,1)} %keys.1) | copy-start | bytes 6291460
  7.2 6.7 %copy-start.4 = (bf16[28,4608]{1,0:T(8,128)(2,1)S(1)}, bf16[28,4608]{1,0:T(8,128)(2,1)}, u32[]{:S(2)}) copy-start(bf16[28,4608]{1,0:T(8,128)(2,1)} %new_qkv.1) | copy-start | bytes 774148
  7.3 6.7 %copy-start.5 = (bf16[28,3584]{1,0:T(8,128)(2,1)S(1)}, bf16[28,3584]{1,0:T(8,128)(2,1)}, u32[]{:S(2)}) copy-start(bf16[28,3584]{1,0:T(8,128)(2,1)} %new_out.1) | copy-start | bytes 602116
  7.3 6.7 %copy-start.6 = (bf16[4,3584]{1,0:T(4,128)(2,1)S(1)}, bf16[4,3584]{1,0:T(4,128)(2,1)}, u32[]{:S(2)}) copy-start(bf16[4,3584]{1,0:T(4,128)(2,1)} %hidden.1) | copy-start | bytes 86020
  7.3 6.7 %copy-start.7 = (s32[4]{0:T(128)S(1)}, s32[4]{0:T(128)}, u32[]{:S(2)}) copy-start(s32[4]{0:T(128)} %len_smem.1) | copy-start | bytes 52
  14.0 1.6 %copy-start.3 = (bf16[4,512,512]{2,1,0:T(8,128)(2,1)S(1)}, bf16[4,512,512]{2,1,0:T(8,128)(2,1)}, u32[]{:S(2)}) copy-start(bf16[4,512,512]{2,1,0:T(8,128)(2,1)} %values.1) | copy-start | bytes 6291460
  74.2 2.1 %copy-start = (bf16[3584,576]{1,0:T(8,128)(2,1)}, bf16[3584,576]{1,0:T(8,128)(2,1)S(1)}, u32[]{:S(2)}) copy-start(bf16[3584,576]{1,0:T(8,128)(2,1)S(1)} %get-tuple-element.14) | copy-start | bytes 12386308
  76.2 1.8 %copy-start.1 = (bf16[3584,448]{1,0:T(8,128)(2,1)}, bf16[3584,448]{1,0:T(8,128)(2,1)S(1)}, u32[]{:S(2)}) copy-start(bf16[3584,448]{1,0:T(8,128)(2,1)S(1)} %get-tuple-element.15) | copy-start | bytes 9633796

commit v2 on v1

--- a/solution.py
+++ b/solution.py
@@ -1,7 +1,6 @@
-import functools
-
 import jax
 import jax.numpy as jnp
+import numpy as np
 from jax import lax
 from jax.experimental import pallas as pl
 from jax.experimental.pallas import tpu as pltpu
@@ -16,7 +15,7 @@
 QC = 576
 OC = 448
 TILES = 8
-SLOT = ROWS * TILES
+QUADS = ROWS // 4
 SEQ = 4
 CHUNK = 512
 PAIRS = SEQ * KVH
@@ -25,13 +24,14 @@
 X_FIRST = (True, True, False, True, False, True, False, True)
 F32 = jnp.float32
 BF16 = jnp.bfloat16
+NT = (((1,), (1,)), ((), ()))
 
 
 def move_kernel(
-    len_smem, hidden, trig, old_qkv, old_out, keys, values, new_qkv, new_out,
+    len_smem, hidden, freq, old_qkv, old_out, keys, values, new_qkv, new_out,
     land, decoded,
-    packed, nq, no, hid, trg, wq, wo, kb, vb,
-    jown, jall, jfull, qf, ownb, part, parts, att, amat, lensem,
+    packed, nq, no, hid, frq, wq, wo, kb, vb,
+    jown, jall, jfull, qf, ownb, part, parts, att, amat,
     load_sem, recv_sem, send_sem, small_recv, small_send,
 ):
     rep = lax.axis_index("rep")
@@ -51,7 +51,7 @@
 
     loads = []
     for n, (src, dst) in enumerate(
-        ((new_qkv, nq), (new_out, no), (hidden, hid), (trig, trg), (old_qkv, wq), (keys, kb), (values, vb), (old_out, wo))
+        ((new_qkv, nq), (new_out, no), (hidden, hid), (freq, frq), (old_qkv, wq), (keys, kb), (values, vb), (old_out, wo))
     ):
         c = pltpu.make_async_copy(src, dst, load_sem.at[n])
         c.start()
@@ -85,16 +85,19 @@
                 v = jnp.concatenate([a[:, 512:576], b[:, 384:448]], axis=1)
             else:
                 v = b[:, 128 * (k - 5) : 128 * (k - 4)]
-            packed[t, ROWS * k : ROWS * (k + 1), :] = v
+            packed[t, k] = v.reshape(QUADS, 4, 128)
     mine = rep * 8 + tp
-    land[mine] = packed[tp]
+    land[:, pl.ds(QUADS * mine, QUADS)] = packed[tp]
     pl.semaphore_wait(barrier, len(friends))
 
     sent = []
+
+    def place(slot):
+        return land.at[:, pl.ds(QUADS * slot, QUADS)]
 
     def put(src, slot, r, t):
         c = pltpu.make_async_remote_copy(
-            src_ref=src, dst_ref=land.at[slot], send_sem=send_sem.at[len(sent)], recv_sem=recv_sem.at[slot],
+            src_ref=src, dst_ref=place(slot), send_sem=send_sem.at[len(sent)], recv_sem=recv_sem.at[slot],
             device_id={"rep": r, "tp": t}, device_id_type=pl.DeviceIdType.MESH,
         )
         c.start()
@@ -102,7 +105,7 @@
 
     def arrived(slot):
         pltpu.make_async_remote_copy(
-            src_ref=land.at[slot], dst_ref=land.at[slot], send_sem=send_sem.at[0], recv_sem=recv_sem.at[slot],
+            src_ref=place(slot), dst_ref=place(slot), send_sem=send_sem.at[0], recv_sem=recv_sem.at[slot],
             device_id={"rep": rep, "tp": tp}, device_id_type=pl.DeviceIdType.MESH,
         ).wait_recv()
 
@@ -118,16 +121,16 @@
             put(packed.at[t], mine, rep_of(z, (x_lo + f) % 2, core), t)
 
     def up(slot):
-        put(land.at[slot], slot, rep_of(z_up, x_lo, core), tp)
+        put(place(slot), slot, rep_of(z_up, x_lo, core), tp)
 
     def down(slot):
-        put(land.at[slot], slot, rep_of(z_dn, x_lo, core), tp)
+        put(place(slot), slot, rep_of(z_dn, x_lo, core), tp)
 
     def across(slot):
-        put(land.at[slot], slot, rep_of(z, x_ot, core), tp)
+        put(place(slot), slot, rep_of(z, x_ot, core), tp)
 
     def twin(slot):
-        put(land.at[slot], slot, rep_of(z, x_lo, 1 - core), tp)
+        put(place(slot), slot, rep_of(z, x_lo, 1 - core), tp)
 
     def step(s):
         if 0 <= s < 8:
@@ -200,7 +203,7 @@
     def project():
         loads[2].wait()
         loads[4].wait()
-        res = jnp.dot(hid[...], wq[...], preferred_element_type=F32).astype(BF16)
+        res = lax.dot_general(hid[...], wq[...], NT, preferred_element_type=F32).astype(BF16)
         jown[0:SEQ, 0:QC] = res
         jall[tp, 0:SEQ, 0:QC] = res
         to_peers(0, lambda t: jown, lambda: jall.at[tp])
@@ -208,10 +211,16 @@
     def rotary():
         from_peers(0, lambda t: jall.at[t])
         loads[3].wait()
+        row = lax.broadcasted_iota(jnp.int32, (8, HD), 0)
+        lane = lax.broadcasted_iota(jnp.int32, (8, HD), 1)
+        pos = jnp.zeros((8, HD), F32)
+        for s in range(SEQ):
+            pos = jnp.where(row == s, len_smem[s].astype(F32), pos)
+        angles = pos * jnp.broadcast_to(frq[0:1, :], (8, HD))
+        cos2 = jnp.cos(angles)[0:SEQ]
+        sin2 = jnp.where(lane < HD // 2, -jnp.sin(angles), jnp.sin(angles))[0:SEQ]
         for t in range(8):
             jfull[0:SEQ, QC * t : QC * (t + 1)] = jall[t, 0:SEQ, 0:QC].astype(F32)
-        cos2 = trg[0:SEQ, :]
-        sin2 = trg[8 : 8 + SEQ, :]
         for h in range(HQ + KVH):
             x = jfull[0:SEQ, HD * h : HD * (h + 1)]
             r = x * cos2 + pltpu.roll(x, HD // 2, 1) * sin2
@@ -237,7 +246,7 @@
         for k in range(KVH):
             q = qf[pl.ds(8 * GROUP * k + s, 8, stride=8), :].astype(BF16)
             sc = lax.dot_general(
-                q, kb[s, :, HD * k : HD * (k + 1)], (((1,), (1,)), ((), ())), preferred_element_type=F32
+                q, kb[s, :, HD * k : HD * (k + 1)], NT, preferred_element_type=F32
             ) * inv_root
             sc = jnp.where(live, sc, F32(-1e30))
             m = jnp.max(sc, axis=1, keepdims=True)
@@ -279,8 +288,8 @@
                 h = GROUP * k + g
                 for s in range(SEQ):
                     amat[s : s + 1, HD * h : HD * (h + 1)] = att[s * KVH + k, g : g + 1, :]
-        decoded[...] = jnp.dot(
-            amat[0:SEQ, :].astype(BF16), wo[...], preferred_element_type=F32
+        decoded[...] = lax.dot_general(
+            amat[0:SEQ, :].astype(BF16), wo[...], NT, preferred_element_type=F32
         ).astype(BF16)
 
     step(0)
@@ -316,65 +325,74 @@
 
 
 def write_kernel(land, dec, out_q, out_o, out_d, oq, oo, sems):
-    parts = 8
-    rows = 3584 // parts
+    eye = jnp.where(
+        lax.broadcasted_iota(jnp.int32, (256, 256), 0) == lax.broadcasted_iota(jnp.int32, (256, 256), 1), 1.0, 0.0
+    ).astype(BF16)
     copies = []
-    d = pltpu.make_async_copy(dec, out_d, sems.at[2 * parts])
+
+    def out(src, dst, first, n):
+        c = pltpu.make_async_copy(src.at[pl.ds(first, n)], dst.at[pl.ds(first, n)], sems.at[len(copies)])
+        c.start()
+        copies.append(c)
+
+    d = pltpu.make_async_copy(dec, out_d, sems.at[6])
     d.start()
-    for p in range(parts):
+    for c in range(4):
 
         def body(i, _):
-            r0 = pl.multiple_of(p * rows + i * 112, 112)
-            tq = oq.at[pl.ds(r0, 112)]
-            to = oo.at[pl.ds(r0, 112)]
-            for m in range(4):
-                b = p * 16 + i * 4 + m
-                for k in range(TILES):
-                    v = land[b, ROWS * k : ROWS * (k + 1), :]
-                    at = pl.ds(ROWS * m, ROWS)
-                    if k < 4:
-                        tq[at, 128 * k : 128 * (k + 1)] = v
-                    elif k == 4:
-                        tq[at, 512:576] = v[:, 0:64]
-                        to[at, 384:448] = v[:, 64:128]
-                    else:
-                        to[at, 128 * (k - 5) : 128 * (k - 4)] = v
+            q0 = i * 64
+            w = jnp.concatenate(
+                [land[2 * c + n, pl.ds(q0, 64)].reshape(256, 128) for n in range(2)], axis=1
+            )
+            v = lax.dot_general(eye, w, NT, preferred_element_type=F32).astype(BF16)
+            at = pl.ds(pl.multiple_of(i * 256, 256), 256)
+            if c < 2:
+                oq[256 * c : 256 * (c + 1), at] = v
+            elif c == 2:
+                oq[512:576, at] = v[0:64]
+                oo[384:448, at] = v[64:128]
+                oo[0:128, at] = v[128:256]
+            else:
+                oo[128:384, at] = v
             return 0
 
-        lax.fori_loop(0, rows // 112, body, 0)
-        for n, (src, dst) in enumerate(((oq, out_q), (oo, out_o))):
-            c = pltpu.make_async_copy(src.at[pl.ds(p * rows, rows)], dst.at[pl.ds(p * rows, rows)], sems.at[2 * p + n])
-            c.start()
-            copies.append(c)
+        lax.fori_loop(0, 14, body, 0)
+        if c < 2:
+            out(oq, out_q, 256 * c, 256)
+        elif c == 2:
+            out(oq, out_q, 512, 64)
+            out(oo, out_o, 384, 64)
+            out(oo, out_o, 0, 128)
+        else:
+            out(oo, out_o, 128, 256)
     for c in copies:
         c.wait()
     d.wait()
 
 
 def per_device(hidden_state, lengths, old_qkv, old_out, cache_keys, cache_values, new_qkv, new_out):
-    half = HD // 2
-    frequency = ROPE_BASE ** (-2.0 * jnp.arange(half, dtype=F32) / (2 * half))
-    angles = lengths.astype(F32)[:, None] * frequency
-    cos, sin = jnp.cos(angles), jnp.sin(angles)
-    pad = jnp.zeros((4, HD), F32)
-    trig = jnp.concatenate(
-        [jnp.concatenate([cos, cos], 1), pad, jnp.concatenate([-sin, sin], 1), pad], 0
-    )
+    half = ROPE_BASE ** (-2.0 * np.arange(HD // 2) / HD)
+    freq = jnp.asarray(np.concatenate([half, half])[None], F32)
     any_ = pl.BlockSpec(memory_space=pl.ANY)
+    hbm = pl.BlockSpec(memory_space=pltpu.HBM)
     vmem = pl.BlockSpec(memory_space=pltpu.VMEM)
+    far = [
+        pltpu.with_memory_space_constraint(a, pltpu.HBM)
+        for a in (hidden_state, freq, old_qkv.T, old_out.T, cache_keys, cache_values, new_qkv, new_out)
+    ]
     land, dec = pl.pallas_call(
         move_kernel,
-        out_shape=(pltpu.VMEM((128, SLOT, 128), BF16), pltpu.VMEM((SEQ, OC), BF16)),
-        in_specs=[pl.BlockSpec(memory_space=pltpu.SMEM)] + [any_] * 8,
+        out_shape=(pltpu.VMEM((TILES, 128 * QUADS, 4, 128), BF16), pltpu.VMEM((SEQ, OC), BF16)),
+        in_specs=[pl.BlockSpec(memory_space=pltpu.SMEM)] + [hbm] * 8,
         out_specs=(vmem, vmem),
         scratch_shapes=[
-            pltpu.VMEM((8, SLOT, 128), BF16),
+            pltpu.VMEM((8, TILES, QUADS, 4, 128), BF16),
             pltpu.VMEM((ROWS, 4608), BF16),
             pltpu.VMEM((ROWS, 3584), BF16),
             pltpu.VMEM((SEQ, 3584), BF16),
-            pltpu.VMEM((16, HD), F32),
-            pltpu.VMEM((3584, QC), BF16),
-            pltpu.VMEM((3584, OC), BF16),
+            pltpu.VMEM((1, HD), F32),
+            pltpu.VMEM((QC, 3584), BF16),
+            pltpu.VMEM((OC, 3584), BF16),
             pltpu.VMEM((SEQ, CHUNK, 512), BF16),
             pltpu.VMEM((SEQ, CHUNK, 512), BF16),
             pltpu.VMEM((16, 640), BF16),
@@ -386,7 +404,6 @@
             pltpu.VMEM((8, 2, 16, HD), F32),
             pltpu.VMEM((PAIRS, 8, HD), F32),
             pltpu.VMEM((8, 3584), F32),
-            pltpu.SemaphoreType.REGULAR,
             pltpu.SemaphoreType.DMA((8,)),
             pltpu.SemaphoreType.DMA((128,)),
             pltpu.SemaphoreType.DMA((128,)),
@@ -397,25 +414,21 @@
             collective_id=0, has_side_effects=True, vmem_limit_bytes=40 * 1024 * 1024
         ),
         name="move",
-    )(lengths, hidden_state, trig, old_qkv, old_out, cache_keys, cache_values, new_qkv, new_out)
+    )(lengths, *far)
     qkv_tp, out_tp, decoded = pl.pallas_call(
         write_kernel,
-        out_shape=(
-            jax.ShapeDtypeStruct((3584, QC), BF16),
-            jax.ShapeDtypeStruct((3584, OC), BF16),
-            jax.ShapeDtypeStruct((SEQ, OC), BF16),
-        ),
+        out_shape=(pltpu.HBM((QC, 3584), BF16), pltpu.HBM((OC, 3584), BF16), pltpu.HBM((SEQ, OC), BF16)),
         in_specs=[vmem, vmem],
-        out_specs=(any_, any_, any_),
+        out_specs=(hbm, hbm, hbm),
         scratch_shapes=[
-            pltpu.VMEM((3584, QC), BF16),
-            pltpu.VMEM((3584, OC), BF16),
-            pltpu.SemaphoreType.DMA((17,)),
+            pltpu.VMEM((QC, 3584), BF16),
+            pltpu.VMEM((OC, 3584), BF16),
+            pltpu.SemaphoreType.DMA((7,)),
         ],
         compiler_params=pltpu.CompilerParams(vmem_limit_bytes=24 * 1024 * 1024),
         name="write",
     )(land, dec)
-    return decoded, qkv_tp, out_tp
+    return decoded, qkv_tp.T, out_tp.T
 
 
 def solution(mesh):

time: 90.8 us -> 66.9 us (0.74)
  local copies, waits for them, and re-layouts: 30.1 us -> 0.65 us
  Pallas kernels: 58.6 us -> 65.5 us
    unnamed x20 -> x2, local copies, waits for them, and re-layouts: 30.1 us -> 0.65 us
    pallas_call x2, Pallas kernels: 58.6 us -> 65.5 us  [the longest x1 51.4 us: per_device(): pl.pallas_call(move_kernel, out_shape=(pltpu.VMEM((TILES, 128 * QUADS, 4,...]
where the time goes in v2:
time: 66.9 us; the launch traced here: 66.8 us
  Pallas kernels  65.5 us (98%)
    pallas_call x1, Pallas kernels, per_device(): pl.pallas_call(move_kernel, out_shape=(pltpu.VMEM((TILES, 128 * QUADS, 4,...  51.4 us
    pallas_call x1, Pallas kernels, per_device(): pl.pallas_call(write_kernel, out_shape=(pltpu.HBM((QC, 3584), BF16), pltp...  14 us

profile of v2, /device:TPU:1, one launch (start us, length us, event | category | flops | bytes accessed | tf_op | source)
XLA Modules:
  0.0 66.8 jit_solution(14209035946420075055)
XLA Ops:
  0.6 0.0 copy-start
  0.6 0.6 copy-done
  1.3 51.4 %move.1 = (bf16[8,896,4,128]{3,2,1,0:T(4,128)(2,1)S(1)}, bf16[4,448]{1,0:T(4,128)(2,1)S(1)}) custom-call(s32[4]{0:T(128)S(1)} %copy-done, bf16[4,3584]{1,0:T(4,128)(2,1)} %hidden.1, f32[1,128]{1,0:T(1,128)} %constant.2.clone.freq, bf16[576,3584]{1,0:T(8,128)(2,1)} %bitcast.4, bf16[448,3584]{1,0:T(8,128)(2,1)} %bitcast.5, bf16[4,512,512]{2,1,0:T(8,128)(2,1)} %keys.1, ...), custom_call_target="tpu_custom_call" | custom-call | tf_op jit(solution)/shard_map/move/pallas_call | solution.py:383
  52.7 14.0 %write.1 = (bf16[576,3584]{1,0:T(8,128)(2,1)}, bf16[448,3584]{1,0:T(8,128)(2,1)}, bf16[4,448]{1,0:T(4,128)(2,1)}) custom-call(bf16[8,896,4,128]{3,2,1,0:T(4,128)(2,1)S(1)} %get-tuple-element.8.land, bf16[4,448]{1,0:T(4,128)(2,1)S(1)} %get-tuple-element.9.dec), custom_call_target="tpu_custom_call" | custom-call | tf_op jit(solution)/shard_map/write/pallas_call | solution.py:418
Async XLA Ops:
  0.6 0.7 copy-start

commit v3 on v2

--- a/solution.py
+++ b/solution.py
@@ -21,18 +21,30 @@
 PAIRS = SEQ * KVH
 
 ITEMS = ((0, 0), (0, 1), (1, 0), (3, 0), (1, 1), (3, 1), (2, 0), (2, 1))
-X_FIRST = (True, True, False, True, False, True, False, True)
+X_FIRST = (False, True, True, True, True, False, False, False)
+ORDER = (
+    ("O", 0), ("O", 1), ("P", 0), ("D", 0), ("U", 0), ("O", 2), ("O", 3), ("O", 4), ("O", 5), ("P", 1), ("D", 1),
+    ("U", 1), ("O", 6), ("d", 0), ("V", 0), ("U", 2), ("O", 7), ("u", 0), ("D", 2), ("U", 3), ("P", 2), ("D", 3),
+    ("U", 4), ("P", 3), ("D", 4), ("U", 5), ("P", 4), ("D", 5), ("V", 1), ("P", 5), ("d", 1), ("u", 1), ("P", 6),
+    ("D", 6), ("U", 6), ("v", 0), ("D", 7), ("U", 7), ("P", 7), ("V", 2), ("V", 3), ("d", 2), ("u", 2), ("u", 5),
+    ("d", 5), ("V", 4), ("V", 5), ("d", 3), ("d", 6), ("u", 3), ("d", 4), ("u", 4), ("u", 6), ("d", 7), ("v", 1),
+    ("V", 7), ("v", 2), ("u", 7), ("V", 6), ("v", 3), ("v", 4), ("v", 5), ("v", 7), ("v", 6),
+)
+DECODE = {
+    ("O", 0): ("exchange", "project"), ("U", 1): ("rotary",), ("U", 2): ("attend0",), ("U", 4): ("attend1",),
+    ("P", 4): ("attend2",), ("P", 6): ("attend3", "share"), ("V", 5): ("combine",), ("d", 7): ("finish",),
+}
 F32 = jnp.float32
 BF16 = jnp.bfloat16
 NT = (((1,), (1,)), ((), ()))
 
 
 def move_kernel(
-    len_smem, hidden, freq, old_qkv, old_out, keys, values, new_qkv, new_out,
+    lengths, hidden, freq, old_qkv, old_out, keys, values, new_qkv, new_out,
     land, decoded,
     packed, nq, no, hid, frq, wq, wo, kb, vb,
     jown, jall, jfull, qf, ownb, part, parts, att, amat,
-    load_sem, recv_sem, send_sem, small_recv, small_send,
+    lens, load_sem, recv_sem, twin_sem, send_sem, small_recv, small_send,
 ):
     rep = lax.axis_index("rep")
     tp = lax.axis_index("tp")
@@ -51,7 +63,7 @@
 
     loads = []
     for n, (src, dst) in enumerate(
-        ((new_qkv, nq), (new_out, no), (hidden, hid), (freq, frq), (old_qkv, wq), (keys, kb), (values, vb), (old_out, wo))
+        ((new_qkv, nq), (new_out, no), (hidden, hid), (freq, frq), (old_qkv, wq), (keys, kb), (values, vb), (old_out, wo), (lengths, lens))
     ):
         c = pltpu.make_async_copy(src, dst, load_sem.at[n])
         c.start()
@@ -92,12 +104,16 @@
 
     sent = []
 
+    def slot_key(slot):
+        return slot // 16 * 8 + slot % 8
+
     def place(slot):
         return land.at[:, pl.ds(QUADS * slot, QUADS)]
 
-    def put(src, slot, r, t):
+    def put(src, slot, r, t, sem=None):
         c = pltpu.make_async_remote_copy(
-            src_ref=src, dst_ref=place(slot), send_sem=send_sem.at[len(sent)], recv_sem=recv_sem.at[slot],
+            src_ref=src, dst_ref=place(slot), send_sem=send_sem.at[0],
+            recv_sem=recv_sem.at[slot_key(slot)] if sem is None else sem,
             device_id={"rep": r, "tp": t}, device_id_type=pl.DeviceIdType.MESH,
         )
         c.start()
@@ -105,7 +121,8 @@
 
     def arrived(slot):
         pltpu.make_async_remote_copy(
-            src_ref=place(slot), dst_ref=place(slot), send_sem=send_sem.at[0], recv_sem=recv_sem.at[slot],
+            src_ref=place(slot), dst_ref=place(slot), send_sem=send_sem.at[0],
+            recv_sem=recv_sem.at[slot_key(slot)],
             device_id={"rep": rep, "tp": tp}, device_id_type=pl.DeviceIdType.MESH,
         ).wait_recv()
 
@@ -129,54 +146,26 @@
     def across(slot):
         put(place(slot), slot, rep_of(z, x_ot, core), tp)
 
-    def twin(slot):
-        put(place(slot), slot, rep_of(z, x_lo, 1 - core), tp)
-
-    def step(s):
-        if 0 <= s < 8:
-            b = slot_of(z, x_lo, ITEMS[s])
-            if s:
-                arrived(b)
-            across(b)
+    def twin(slot, j):
+        put(place(slot), slot, rep_of(z, x_lo, 1 - core), tp, twin_sem.at[j])
+
+    def handle(kind, j):
+        first, fwd_up = X_FIRST[j], j % 2 == 0
+        zz = {"o": z, "p": z, "d": z_dn, "u": z_up, "v": z_op}[kind.lower()]
+        xx = x_lo if kind in "ODUV" else x_ot
+        b = slot_of(zz, xx, ITEMS[j])
+        if (kind, j) != ("O", 0):
+            arrived(b)
+        if kind == "O" or (kind == "P" and first):
             up(b)
             down(b)
-            twin(b)
-        j = s - 1
-        if 0 <= j < 8:
-            it = ITEMS[j]
-            b = slot_of(z, x_ot, it)
-            arrived(b)
-            if X_FIRST[j]:
-                up(b)
-                down(b)
-            twin(b)
-            for zz, go, fwd in ((z_dn, up, j % 2 == 0), (z_up, down, j % 2 == 1)):
-                b = slot_of(zz, x_lo, it)
-                arrived(b)
-                if fwd:
-                    go(b)
-                if not X_FIRST[j]:
-                    across(b)
-                twin(b)
-        j = s - 2
-        if 0 <= j < 8:
-            it = ITEMS[j]
-            for zz, go, fwd in ((z_dn, up, j % 2 == 1), (z_up, down, j % 2 == 0)):
-                b = slot_of(zz, x_ot, it)
-                arrived(b)
-                if fwd and X_FIRST[j]:
-                    go(b)
-                twin(b)
-            b = slot_of(z_op, x_lo, it)
-            arrived(b)
-            if not X_FIRST[j]:
-                across(b)
-            twin(b)
-        j = s - 3
-        if 0 <= j < 8:
-            b = slot_of(z_op, x_ot, ITEMS[j])
-            arrived(b)
-            twin(b)
+        if (kind == "D" and fwd_up) or (kind == "d" and first and not fwd_up):
+            up(b)
+        if (kind == "U" and not fwd_up) or (kind == "u" and first and fwd_up):
+            down(b)
+        if kind == "O" or (kind in "DUV" and not first):
+            across(b)
+        twin(b, j)
 
     small = []
 
@@ -184,21 +173,17 @@
         for n in range(1, 8):
             t = (tp + n) % 8
             c = pltpu.make_async_remote_copy(
-                src_ref=src_of(t), dst_ref=dst_of(), send_sem=small_send.at[phase, n - 1],
-                recv_sem=small_recv.at[phase, tp],
+                src_ref=src_of(t), dst_ref=dst_of(), send_sem=small_send.at[phase],
+                recv_sem=small_recv.at[phase],
                 device_id={"rep": rep, "tp": t}, device_id_type=pl.DeviceIdType.MESH,
             )
             c.start()
             small.append(c)
 
-    def from_peers(phase, dst_from):
-        for n in range(1, 8):
-            t = (tp + 8 - n) % 8
-            pltpu.make_async_remote_copy(
-                src_ref=dst_from(t), dst_ref=dst_from(t), send_sem=small_send.at[phase, 0],
-                recv_sem=small_recv.at[phase, t],
-                device_id={"rep": rep, "tp": tp}, device_id_type=pl.DeviceIdType.MESH,
-            ).wait_recv()
+    def all_bytes(ref, sem):
+        pltpu.make_async_copy(ref, ref, sem).wait()
+
+    seven = (jall.at[pl.ds(0, 7)], parts.at[pl.ds(0, 7)], att.at[pl.ds(0, 7 * 16)])
 
     def project():
         loads[2].wait()
@@ -209,13 +194,14 @@
         to_peers(0, lambda t: jown, lambda: jall.at[tp])
 
     def rotary():
-        from_peers(0, lambda t: jall.at[t])
+        all_bytes(seven[0], small_recv.at[0])
         loads[3].wait()
+        loads[8].wait()
         row = lax.broadcasted_iota(jnp.int32, (8, HD), 0)
         lane = lax.broadcasted_iota(jnp.int32, (8, HD), 1)
         pos = jnp.zeros((8, HD), F32)
         for s in range(SEQ):
-            pos = jnp.where(row == s, len_smem[s].astype(F32), pos)
+            pos = jnp.where(row == s, lens[s].astype(F32), pos)
         angles = pos * jnp.broadcast_to(frq[0:1, :], (8, HD))
         cos2 = jnp.cos(angles)[0:SEQ]
         sin2 = jnp.where(lane < HD // 2, -jnp.sin(angles), jnp.sin(angles))[0:SEQ]
@@ -241,7 +227,7 @@
             loads[6].wait()
         inv_root = 1.0 / jnp.sqrt(F32(HD))
         pos = lax.broadcasted_iota(jnp.int32, (8, CHUNK), 1) + tp * CHUNK
-        live = pos < len_smem[s]
+        live = pos < lens[s]
         lane = lax.broadcasted_iota(jnp.int32, (8, HD), 1)
         for k in range(KVH):
             q = qf[pl.ds(8 * GROUP * k + s, 8, stride=8), :].astype(BF16)
@@ -263,7 +249,7 @@
         to_peers(1, lambda t: part.at[pl.ds(2 * t, 2)], lambda: parts.at[tp])
 
     def combine():
-        from_peers(1, lambda t: parts.at[t])
+        all_bytes(seven[1], small_recv.at[1])
         for n in range(2):
             own = ownb[2 * tp + n, 0:8, :]
             val = ownb[2 * tp + n, 8:16, :]
@@ -277,51 +263,34 @@
                 scale = jnp.exp(jnp.broadcast_to(parts[t, n, 8:16, 0:1], (8, HD)) - top)
                 num = num + parts[t, n, 0:8, :] * scale
                 den = den + jnp.broadcast_to(parts[t, n, 8:16, 1:2], (8, HD)) * scale
-            att[2 * tp + n] = (num / den).astype(BF16).astype(F32)
-        to_peers(2, lambda t: att.at[pl.ds(2 * tp, 2)], lambda: att.at[pl.ds(2 * tp, 2)])
+            att[pl.ds(pl.multiple_of(16 * tp + 8 * n, 8), 8), :] = (num / den).astype(BF16).astype(F32)
+        own = att.at[pl.ds(pl.multiple_of(16 * tp, 16), 16)]
+        to_peers(2, lambda t: own, lambda: own)
 
     def finish():
-        from_peers(2, lambda t: att.at[pl.ds(2 * t, 2)])
+        all_bytes(seven[2], small_recv.at[2])
         loads[7].wait()
         for k in range(KVH):
             for g in range(GROUP):
                 h = GROUP * k + g
-                for s in range(SEQ):
-                    amat[s : s + 1, HD * h : HD * (h + 1)] = att[s * KVH + k, g : g + 1, :]
+                amat[0:SEQ, HD * h : HD * (h + 1)] = att[pl.ds(8 * k + g, SEQ, stride=8 * KVH), :]
         decoded[...] = lax.dot_general(
             amat[0:SEQ, :].astype(BF16), wo[...], NT, preferred_element_type=F32
         ).astype(BF16)
 
-    step(0)
-    exchange()
-    project()
-    step(1)
-    step(2)
-    rotary()
-    step(3)
-    attend(0)
-    attend(1)
-    step(4)
-    attend(2)
-    attend(3)
-    share()
-    step(5)
-    step(6)
-    combine()
-    step(7)
-    step(8)
-    finish()
-    step(9)
-    step(10)
-    for it in ITEMS:
-        for zz in (z, z_dn, z_up, z_op):
-            for xx in (x_lo, x_ot):
-                b = slot_of(zz, xx, it)
-                arrived(b + 8 * (1 - 2 * core))
-    for c in sent:
-        c.wait_send()
-    for c in small:
-        c.wait_send()
+    pieces = {"exchange": exchange, "project": project, "rotary": rotary, "share": share, "combine": combine, "finish": finish}
+    for event in ORDER:
+        handle(*event)
+        for piece in DECODE.get(event, ()):
+            if piece.startswith("attend"):
+                attend(int(piece[-1]))
+            else:
+                pieces[piece]()
+    for j in range(8):
+        all_bytes(packed, twin_sem.at[j])
+    all_bytes(land.at[:, pl.ds(0, QUADS * len(sent))], send_sem.at[0])
+    for phase in range(3):
+        all_bytes(seven[phase], small_send.at[phase])
 
 
 def write_kernel(land, dec, out_q, out_o, out_d, oq, oo, sems):
@@ -378,12 +347,12 @@
     vmem = pl.BlockSpec(memory_space=pltpu.VMEM)
     far = [
         pltpu.with_memory_space_constraint(a, pltpu.HBM)
-        for a in (hidden_state, freq, old_qkv.T, old_out.T, cache_keys, cache_values, new_qkv, new_out)
+        for a in (lengths, hidden_state, freq, old_qkv.T, old_out.T, cache_keys, cache_values, new_qkv, new_out)
     ]
     land, dec = pl.pallas_call(
         move_kernel,
         out_shape=(pltpu.VMEM((TILES, 128 * QUADS, 4, 128), BF16), pltpu.VMEM((SEQ, OC), BF16)),
-        in_specs=[pl.BlockSpec(memory_space=pltpu.SMEM)] + [hbm] * 8,
+        in_specs=[hbm] * 9,
         out_specs=(vmem, vmem),
         scratch_shapes=[
             pltpu.VMEM((8, TILES, QUADS, 4, 128), BF16),
@@ -402,19 +371,21 @@
             pltpu.VMEM((PAIRS, 16, HD), F32),
             pltpu.VMEM((PAIRS, 16, HD), F32),
             pltpu.VMEM((8, 2, 16, HD), F32),
-            pltpu.VMEM((PAIRS, 8, HD), F32),
+            pltpu.VMEM((PAIRS * 8, HD), F32),
             pltpu.VMEM((8, 3584), F32),
+            pltpu.SMEM((SEQ,), jnp.int32),
+            pltpu.SemaphoreType.DMA((9,)),
+            pltpu.SemaphoreType.DMA((64,)),
             pltpu.SemaphoreType.DMA((8,)),
-            pltpu.SemaphoreType.DMA((128,)),
-            pltpu.SemaphoreType.DMA((128,)),
-            pltpu.SemaphoreType.DMA((3, 8)),
-            pltpu.SemaphoreType.DMA((3, 7)),
+            pltpu.SemaphoreType.DMA((1,)),
+            pltpu.SemaphoreType.DMA((3,)),
+            pltpu.SemaphoreType.DMA((3,)),
         ],
         compiler_params=pltpu.CompilerParams(
             collective_id=0, has_side_effects=True, vmem_limit_bytes=40 * 1024 * 1024
         ),
         name="move",
-    )(lengths, *far)
+    )(*far)
     qkv_tp, out_tp, decoded = pl.pallas_call(
         write_kernel,
         out_shape=(pltpu.HBM((QC, 3584), BF16), pltpu.HBM((OC, 3584), BF16), pltpu.HBM((SEQ, OC), BF16)),

time: 66.9 us -> 59.6 us (0.89)
  Pallas kernels: 65.5 us -> 58.8 us
    pallas_call x1, Pallas kernels: 51.4 us -> 44.8 us  [per_device(): pl.pallas_call(move_kernel, out_shape=(pltpu.VMEM((TILES, 128 * QUADS, 4,...]
where the time goes in v3:
time: 59.6 us; the launch traced here: 59.4 us
  Pallas kernels  58.8 us (99%)
  between operations  0.64 us (1%)
    pallas_call x1, Pallas kernels, per_device(): pl.pallas_call(move_kernel, out_shape=(pltpu.VMEM((TILES, 128 * QUADS, 4,...  44.8 us
    pallas_call x1, Pallas kernels, per_device(): pl.pallas_call(write_kernel, out_shape=(pltpu.HBM((QC, 3584), BF16), pltp...  14 us

profile of v3, /device:TPU:1, one launch (start us, length us, event | category | flops | bytes accessed | tf_op | source)
XLA Modules:
  0.0 59.4 jit_solution(12290391180254248848)
XLA Ops:
  0.6 44.8 %move.1 = (bf16[8,896,4,128]{3,2,1,0:T(4,128)(2,1)S(1)}, bf16[4,448]{1,0:T(4,128)(2,1)S(1)}) custom-call(s32[4]{0:T(128)} %lengths.1, bf16[4,3584]{1,0:T(4,128)(2,1)} %hidden.1, f32[1,128]{1,0:T(1,128)} %constant.2.clone.freq, bf16[576,3584]{1,0:T(8,128)(2,1)} %bitcast.4, bf16[448,3584]{1,0:T(8,128)(2,1)} %bitcast.5, bf16[4,512,512]{2,1,0:T(8,128)(2,1)} %keys.1, ...), custom_call_target="tpu_custom_call" | custom-call | tf_op jit(solution)/shard_map/move/pallas_call | solution.py:352
  45.4 14.0 %write.1 = (bf16[576,3584]{1,0:T(8,128)(2,1)}, bf16[448,3584]{1,0:T(8,128)(2,1)}, bf16[4,448]{1,0:T(4,128)(2,1)}) custom-call(bf16[8,896,4,128]{3,2,1,0:T(4,128)(2,1)S(1)} %get-tuple-element.8.land, bf16[4,448]{1,0:T(4,128)(2,1)S(1)} %get-tuple-element.9.dec), custom_call_target="tpu_custom_call" | custom-call | tf_op jit(solution)/shard_map/write/pallas_call | solution.py:389

commit v4 on v3

--- a/solution.py
+++ b/solution.py
@@ -17,6 +17,7 @@
 TILES = 8
 QUADS = ROWS // 4
 SEQ = 4
+WIDE = 896
 CHUNK = 512
 PAIRS = SEQ * KVH
 
@@ -294,9 +295,6 @@
 
 
 def write_kernel(land, dec, out_q, out_o, out_d, oq, oo, sems):
-    eye = jnp.where(
-        lax.broadcasted_iota(jnp.int32, (256, 256), 0) == lax.broadcasted_iota(jnp.int32, (256, 256), 1), 1.0, 0.0
-    ).astype(BF16)
     copies = []
 
     def out(src, dst, first, n):
@@ -304,36 +302,30 @@
         c.start()
         copies.append(c)
 
-    d = pltpu.make_async_copy(dec, out_d, sems.at[6])
+    d = pltpu.make_async_copy(dec, out_d, sems.at[9])
     d.start()
-    for c in range(4):
+    for k in range(TILES):
 
         def body(i, _):
-            q0 = i * 64
-            w = jnp.concatenate(
-                [land[2 * c + n, pl.ds(q0, 64)].reshape(256, 128) for n in range(2)], axis=1
-            )
-            v = lax.dot_general(eye, w, NT, preferred_element_type=F32).astype(BF16)
-            at = pl.ds(pl.multiple_of(i * 256, 256), 256)
-            if c < 2:
-                oq[256 * c : 256 * (c + 1), at] = v
-            elif c == 2:
+            v = land[k, pl.ds(i * (WIDE // 4), WIDE // 4)].reshape(WIDE, 128).T
+            at = pl.ds(pl.multiple_of(i * WIDE, WIDE), WIDE)
+            if k < 4:
+                oq[128 * k : 128 * (k + 1), at] = v
+            elif k == 4:
                 oq[512:576, at] = v[0:64]
                 oo[384:448, at] = v[64:128]
-                oo[0:128, at] = v[128:256]
             else:
-                oo[128:384, at] = v
+                oo[128 * (k - 5) : 128 * (k - 4), at] = v
             return 0
 
-        lax.fori_loop(0, 14, body, 0)
-        if c < 2:
-            out(oq, out_q, 256 * c, 256)
-        elif c == 2:
+        lax.fori_loop(0, 3584 // WIDE, body, 0)
+        if k < 4:
+            out(oq, out_q, 128 * k, 128)
+        elif k == 4:
             out(oq, out_q, 512, 64)
             out(oo, out_o, 384, 64)
-            out(oo, out_o, 0, 128)
         else:
-            out(oo, out_o, 128, 256)
+            out(oo, out_o, 128 * (k - 5), 128)
     for c in copies:
         c.wait()
     d.wait()
@@ -394,7 +386,7 @@
         scratch_shapes=[
             pltpu.VMEM((QC, 3584), BF16),
             pltpu.VMEM((OC, 3584), BF16),
-            pltpu.SemaphoreType.DMA((7,)),
+            pltpu.SemaphoreType.DMA((10,)),
         ],
         compiler_params=pltpu.CompilerParams(vmem_limit_bytes=24 * 1024 * 1024),
         name="write",

time: 59.6 us -> 50.6 us (0.85)
  Pallas kernels: 58.8 us -> 49.8 us
    pallas_call x1, Pallas kernels: 14 us -> 5.05 us  [per_device(): pl.pallas_call(write_kernel, out_shape=(pltpu.HBM((QC, 3584), BF16), pltp...]
where the time goes in v4:
time: 50.6 us; the launch traced here: 50.5 us
  Pallas kernels  49.8 us (98%)
  between operations  0.64 us (1%)
    pallas_call x1, Pallas kernels, per_device(): pl.pallas_call(move_kernel, out_shape=(pltpu.VMEM((TILES, 128 * QUADS, 4,...  44.8 us
    pallas_call x1, Pallas kernels, per_device(): pl.pallas_call(write_kernel, out_shape=(pltpu.HBM((QC, 3584), BF16), pltp...  5.05 us

profile of v4, /device:TPU:1, one launch (start us, length us, event | category | flops | bytes accessed | tf_op | source)
XLA Modules:
  0.0 50.5 jit_solution(2497483992480762745)
XLA Ops:
  0.6 44.8 %move.1 = (bf16[8,896,4,128]{3,2,1,0:T(4,128)(2,1)S(1)}, bf16[4,448]{1,0:T(4,128)(2,1)S(1)}) custom-call(s32[4]{0:T(128)} %lengths.1, bf16[4,3584]{1,0:T(4,128)(2,1)} %hidden.1, f32[1,128]{1,0:T(1,128)} %constant.2.clone.freq, bf16[576,3584]{1,0:T(8,128)(2,1)} %bitcast.4, bf16[448,3584]{1,0:T(8,128)(2,1)} %bitcast.5, bf16[4,512,512]{2,1,0:T(8,128)(2,1)} %keys.1, ...), custom_call_target="tpu_custom_call" | custom-call | tf_op jit(solution)/shard_map/move/pallas_call | solution.py:344
  45.4 5.1 %write.1 = (bf16[576,3584]{1,0:T(8,128)(2,1)}, bf16[448,3584]{1,0:T(8,128)(2,1)}, bf16[4,448]{1,0:T(4,128)(2,1)}) custom-call(bf16[8,896,4,128]{3,2,1,0:T(4,128)(2,1)S(1)} %get-tuple-element.8.land, bf16[4,448]{1,0:T(4,128)(2,1)S(1)} %get-tuple-element.9.dec), custom_call_target="tpu_custom_call" | custom-call | tf_op jit(solution)/shard_map/write/pallas_call | solution.py:381

commit v5 on v4

--- a/solution.py
+++ b/solution.py
@@ -17,23 +17,23 @@
 TILES = 8
 QUADS = ROWS // 4
 SEQ = 4
-WIDE = 896
 CHUNK = 512
 PAIRS = SEQ * KVH
 
 ITEMS = ((0, 0), (0, 1), (1, 0), (3, 0), (1, 1), (3, 1), (2, 0), (2, 1))
-X_FIRST = (False, True, True, True, True, False, False, False)
+X_FIRST = (False, False, True, True, True, True, True, False)
+PASS_UP = (True, False, True, False, True, False, True, True)
 ORDER = (
     ("O", 0), ("O", 1), ("P", 0), ("D", 0), ("U", 0), ("O", 2), ("O", 3), ("O", 4), ("O", 5), ("P", 1), ("D", 1),
     ("U", 1), ("O", 6), ("d", 0), ("V", 0), ("U", 2), ("O", 7), ("u", 0), ("D", 2), ("U", 3), ("P", 2), ("D", 3),
-    ("U", 4), ("P", 3), ("D", 4), ("U", 5), ("P", 4), ("D", 5), ("V", 1), ("P", 5), ("d", 1), ("u", 1), ("P", 6),
-    ("D", 6), ("U", 6), ("v", 0), ("D", 7), ("U", 7), ("P", 7), ("V", 2), ("V", 3), ("d", 2), ("u", 2), ("u", 5),
-    ("d", 5), ("V", 4), ("V", 5), ("d", 3), ("d", 6), ("u", 3), ("d", 4), ("u", 4), ("u", 6), ("d", 7), ("v", 1),
-    ("V", 7), ("v", 2), ("u", 7), ("V", 6), ("v", 3), ("v", 4), ("v", 5), ("v", 7), ("v", 6),
+    ("U", 4), ("P", 3), ("D", 4), ("U", 5), ("P", 4), ("D", 5), ("V", 1), ("P", 5), ("D", 6), ("U", 6), ("d", 1),
+    ("D", 7), ("U", 7), ("u", 1), ("V", 2), ("V", 3), ("P", 6), ("d", 2), ("u", 2), ("v", 0), ("V", 4), ("V", 5),
+    ("P", 7), ("d", 3), ("u", 3), ("d", 4), ("u", 4), ("v", 1), ("u", 5), ("V", 6), ("d", 7), ("d", 5), ("v", 2),
+    ("u", 7), ("u", 6), ("V", 7), ("d", 6), ("v", 4), ("v", 3), ("v", 6), ("v", 7), ("v", 5),
 )
 DECODE = {
-    ("O", 0): ("exchange", "project"), ("U", 1): ("rotary",), ("U", 2): ("attend0",), ("U", 4): ("attend1",),
-    ("P", 4): ("attend2",), ("P", 6): ("attend3", "share"), ("V", 5): ("combine",), ("d", 7): ("finish",),
+    ("O", 0): ("exchange", "project"), ("U", 1): ("rotary", "attend0"), ("V", 0): ("attend1",), ("U", 2): ("attend2",),
+    ("O", 7): ("attend3", "share"), ("P", 6): ("combine",), ("V", 7): ("finish",),
 }
 F32 = jnp.float32
 BF16 = jnp.bfloat16
@@ -44,7 +44,7 @@
     lengths, hidden, freq, old_qkv, old_out, keys, values, new_qkv, new_out,
     land, decoded,
     packed, nq, no, hid, frq, wq, wo, kb, vb,
-    jown, jall, jfull, qf, ownb, part, parts, att, amat,
+    jown, jall, jfull, qf, ownb, part, parts, att, attf, amat,
     lens, load_sem, recv_sem, twin_sem, send_sem, small_recv, small_send,
 ):
     rep = lax.axis_index("rep")
@@ -151,7 +151,7 @@
         put(place(slot), slot, rep_of(z, x_lo, 1 - core), tp, twin_sem.at[j])
 
     def handle(kind, j):
-        first, fwd_up = X_FIRST[j], j % 2 == 0
+        first, fwd_up = X_FIRST[j], PASS_UP[j]
         zz = {"o": z, "p": z, "d": z_dn, "u": z_up, "v": z_op}[kind.lower()]
         xx = x_lo if kind in "ODUV" else x_ot
         b = slot_of(zz, xx, ITEMS[j])
@@ -190,8 +190,8 @@
         loads[2].wait()
         loads[4].wait()
         res = lax.dot_general(hid[...], wq[...], NT, preferred_element_type=F32).astype(BF16)
-        jown[0:SEQ, 0:QC] = res
-        jall[tp, 0:SEQ, 0:QC] = res
+        jown[:, 0:QC] = res
+        jall[tp, :, 0:QC] = res
         to_peers(0, lambda t: jown, lambda: jall.at[tp])
 
     def rotary():
@@ -207,7 +207,7 @@
         cos2 = jnp.cos(angles)[0:SEQ]
         sin2 = jnp.where(lane < HD // 2, -jnp.sin(angles), jnp.sin(angles))[0:SEQ]
         for t in range(8):
-            jfull[0:SEQ, QC * t : QC * (t + 1)] = jall[t, 0:SEQ, 0:QC].astype(F32)
+            jfull[0:SEQ, QC * t : QC * (t + 1)] = jall[t, :, 0:QC].astype(F32)
         for h in range(HQ + KVH):
             x = jfull[0:SEQ, HD * h : HD * (h + 1)]
             r = x * cos2 + pltpu.roll(x, HD // 2, 1) * sin2
@@ -229,6 +229,7 @@
         inv_root = 1.0 / jnp.sqrt(F32(HD))
         pos = lax.broadcasted_iota(jnp.int32, (8, CHUNK), 1) + tp * CHUNK
         live = pos < lens[s]
+        row = lax.broadcasted_iota(jnp.int32, (8, HD), 0)
         lane = lax.broadcasted_iota(jnp.int32, (8, HD), 1)
         for k in range(KVH):
             q = qf[pl.ds(8 * GROUP * k + s, 8, stride=8), :].astype(BF16)
@@ -240,10 +241,13 @@
             p = jnp.where(live, jnp.exp(sc - m), F32(0.0)).astype(BF16)
             l = jnp.sum(p.astype(F32), axis=1, keepdims=True)
             n = jnp.dot(p, vb[s, :, HD * k : HD * (k + 1)], preferred_element_type=F32)
-            part[s * KVH + k, 0:8, :] = n
-            part[s * KVH + k, 8:16, :] = jnp.where(
-                lane == 0, jnp.broadcast_to(m, (8, HD)), jnp.broadcast_to(l, (8, HD))
+            stats = jnp.sum(
+                jnp.where(lane == row, jnp.broadcast_to(m, (8, HD)), 0.0)
+                + jnp.where(lane == row + 8, jnp.broadcast_to(l, (8, HD)), 0.0),
+                axis=0,
+                keepdims=True,
             )
+            part[s * KVH + k] = jnp.where(row < GROUP, n, jnp.broadcast_to(stats, (8, HD)))
 
     def share():
         parts[tp] = part[pl.ds(2 * tp, 2)]
@@ -251,30 +255,41 @@
 
     def combine():
         all_bytes(seven[1], small_recv.at[1])
+        row = lax.broadcasted_iota(jnp.int32, (8, HD), 0)
+        lane = lax.broadcasted_iota(jnp.int32, (8, HD), 1)
+        done = []
         for n in range(2):
             own = ownb[2 * tp + n, 0:8, :]
             val = ownb[2 * tp + n, 8:16, :]
+            maxima, totals = [], []
             top = own
             for t in range(8):
-                top = jnp.maximum(top, jnp.broadcast_to(parts[t, n, 8:16, 0:1], (8, HD)))
+                stats = jnp.broadcast_to(parts[t, n, GROUP : GROUP + 1, :], (8, HD))
+                m = jnp.sum(jnp.where(lane == row, stats, 0.0), axis=1, keepdims=True)
+                l = jnp.sum(jnp.where(lane == row + 8, stats, 0.0), axis=1, keepdims=True)
+                maxima.append(jnp.broadcast_to(m, (8, HD)))
+                totals.append(jnp.broadcast_to(l, (8, HD)))
+                top = jnp.maximum(top, maxima[t])
             w = jnp.exp(own - top).astype(BF16).astype(F32)
             num = w * val
             den = w
             for t in range(8):
-                scale = jnp.exp(jnp.broadcast_to(parts[t, n, 8:16, 0:1], (8, HD)) - top)
-                num = num + parts[t, n, 0:8, :] * scale
-                den = den + jnp.broadcast_to(parts[t, n, 8:16, 1:2], (8, HD)) * scale
-            att[pl.ds(pl.multiple_of(16 * tp + 8 * n, 8), 8), :] = (num / den).astype(BF16).astype(F32)
+                scale = jnp.exp(maxima[t] - top)
+                num = num + parts[t, n] * scale
+                den = den + totals[t] * scale
+            done.append(num / den)
+        att[pl.ds(pl.multiple_of(16 * tp, 16), 16), :] = jnp.concatenate(done, axis=0).astype(BF16)
         own = att.at[pl.ds(pl.multiple_of(16 * tp, 16), 16)]
         to_peers(2, lambda t: own, lambda: own)
 
     def finish():
         all_bytes(seven[2], small_recv.at[2])
         loads[7].wait()
+        attf[...] = att[...].astype(F32)
         for k in range(KVH):
             for g in range(GROUP):
                 h = GROUP * k + g
-                amat[0:SEQ, HD * h : HD * (h + 1)] = att[pl.ds(8 * k + g, SEQ, stride=8 * KVH), :]
+                amat[0:SEQ, HD * h : HD * (h + 1)] = attf[pl.ds(8 * k + g, SEQ, stride=8 * KVH), :]
         decoded[...] = lax.dot_general(
             amat[0:SEQ, :].astype(BF16), wo[...], NT, preferred_element_type=F32
         ).astype(BF16)
@@ -305,20 +320,14 @@
     d = pltpu.make_async_copy(dec, out_d, sems.at[9])
     d.start()
     for k in range(TILES):
-
-        def body(i, _):
-            v = land[k, pl.ds(i * (WIDE // 4), WIDE // 4)].reshape(WIDE, 128).T
-            at = pl.ds(pl.multiple_of(i * WIDE, WIDE), WIDE)
-            if k < 4:
-                oq[128 * k : 128 * (k + 1), at] = v
-            elif k == 4:
-                oq[512:576, at] = v[0:64]
-                oo[384:448, at] = v[64:128]
-            else:
-                oo[128 * (k - 5) : 128 * (k - 4), at] = v
-            return 0
-
-        lax.fori_loop(0, 3584 // WIDE, body, 0)
+        v = land[k].T
+        if k < 4:
+            oq[128 * k : 128 * (k + 1)] = v
+        elif k == 4:
+            oq[512:576] = v[0:64]
+            oo[384:448] = v[64:128]
+        else:
+            oo[128 * (k - 5) : 128 * (k - 4)] = v
         if k < 4:
             out(oq, out_q, 128 * k, 128)
         elif k == 4:
@@ -356,13 +365,14 @@
             pltpu.VMEM((OC, 3584), BF16),
             pltpu.VMEM((SEQ, CHUNK, 512), BF16),
             pltpu.VMEM((SEQ, CHUNK, 512), BF16),
-            pltpu.VMEM((16, 640), BF16),
-            pltpu.VMEM((8, 16, 640), BF16),
+            pltpu.VMEM((SEQ, 640), BF16),
+            pltpu.VMEM((8, SEQ, 640), BF16),
             pltpu.VMEM((8, 4608), F32),
             pltpu.VMEM((8 * (HQ + KVH), HD), F32),
             pltpu.VMEM((PAIRS, 16, HD), F32),
-            pltpu.VMEM((PAIRS, 16, HD), F32),
-            pltpu.VMEM((8, 2, 16, HD), F32),
+            pltpu.VMEM((PAIRS, 8, HD), F32),
+            pltpu.VMEM((8, 2, 8, HD), F32),
+            pltpu.VMEM((PAIRS * 8, HD), BF16),
             pltpu.VMEM((PAIRS * 8, HD), F32),
             pltpu.VMEM((8, 3584), F32),
             pltpu.SMEM((SEQ,), jnp.int32),
@@ -390,7 +400,7 @@
         ],
         compiler_params=pltpu.CompilerParams(vmem_limit_bytes=24 * 1024 * 1024),
         name="write",
-    )(land, dec)
+    )(land.reshape(TILES, 3584, 128), dec)
     return decoded, qkv_tp.T, out_tp.T
 
 

time: 50.6 us -> 44.1 us (0.87)
  Pallas kernels: 49.8 us -> 43.4 us
    pallas_call x1, Pallas kernels: 44.8 us -> 40 us  [per_device(): pl.pallas_call(move_kernel, out_shape=(pltpu.VMEM((TILES, 128 * QUADS, 4,...]
    pallas_call x1, Pallas kernels: 5.05 us -> 3.36 us  [per_device(): pl.pallas_call(write_kernel, out_shape=(pltpu.HBM((QC, 3584), BF16), pltp...]
where the time goes in v5:
time: 44.1 us; the launch traced here: 44 us
  Pallas kernels  43.4 us (98%)
  between operations  0.64 us (1%)
    pallas_call x1, Pallas kernels, per_device(): pl.pallas_call(move_kernel, out_shape=(pltpu.VMEM((TILES, 128 * QUADS, 4,...  40 us
    pallas_call x1, Pallas kernels, per_device(): pl.pallas_call(write_kernel, out_shape=(pltpu.HBM((QC, 3584), BF16), pltp...  3.36 us

profile of v5, /device:TPU:1, one launch (start us, length us, event | category | flops | bytes accessed | tf_op | source)
XLA Modules:
  0.0 44.0 jit_solution(1202085757482549160)
XLA Ops:
  0.6 40.0 %move.1 = (bf16[8,896,4,128]{3,2,1,0:T(4,128)(2,1)S(1)}, bf16[4,448]{1,0:T(4,128)(2,1)S(1)}) custom-call(s32[4]{0:T(128)} %lengths.1, bf16[4,3584]{1,0:T(4,128)(2,1)} %hidden.1, f32[1,128]{1,0:T(1,128)} %constant.2.clone.freq, bf16[576,3584]{1,0:T(8,128)(2,1)} %bitcast.6, bf16[448,3584]{1,0:T(8,128)(2,1)} %bitcast.7, bf16[4,512,512]{2,1,0:T(8,128)(2,1)} %keys.1, ...), custom_call_target="tpu_custom_call" | custom-call | tf_op jit(solution)/shard_map/move/pallas_call | solution.py:353
  40.7 3.4 %write.1 = (bf16[576,3584]{1,0:T(8,128)(2,1)}, bf16[448,3584]{1,0:T(8,128)(2,1)}, bf16[4,448]{1,0:T(4,128)(2,1)}) custom-call(bf16[8,3584,128]{2,1,0:T(8,128)(2,1)S(1)} %bitcast.5, bf16[4,448]{1,0:T(4,128)(2,1)S(1)} %get-tuple-element.9.dec), custom_call_target="tpu_custom_call" | custom-call | tf_op jit(solution)/shard_map/write/pallas_call | solution.py:391

commit v6 on v5

--- a/solution.py
+++ b/solution.py
@@ -21,19 +21,23 @@
 PAIRS = SEQ * KVH
 
 ITEMS = ((0, 0), (0, 1), (1, 0), (3, 0), (1, 1), (3, 1), (2, 0), (2, 1))
-X_FIRST = (False, False, True, True, True, True, True, False)
+ROUTE = "AACCAABA"
 PASS_UP = (True, False, True, False, True, False, True, True)
 ORDER = (
-    ("O", 0), ("O", 1), ("P", 0), ("D", 0), ("U", 0), ("O", 2), ("O", 3), ("O", 4), ("O", 5), ("P", 1), ("D", 1),
-    ("U", 1), ("O", 6), ("d", 0), ("V", 0), ("U", 2), ("O", 7), ("u", 0), ("D", 2), ("U", 3), ("P", 2), ("D", 3),
-    ("U", 4), ("P", 3), ("D", 4), ("U", 5), ("P", 4), ("D", 5), ("V", 1), ("P", 5), ("D", 6), ("U", 6), ("d", 1),
-    ("D", 7), ("U", 7), ("u", 1), ("V", 2), ("V", 3), ("P", 6), ("d", 2), ("u", 2), ("v", 0), ("V", 4), ("V", 5),
-    ("P", 7), ("d", 3), ("u", 3), ("d", 4), ("u", 4), ("v", 1), ("u", 5), ("V", 6), ("d", 7), ("d", 5), ("v", 2),
-    ("u", 7), ("u", 6), ("V", 7), ("d", 6), ("v", 4), ("v", 3), ("v", 6), ("v", 7), ("v", 5),
+    ("O", 0), ("O", 1), ("D", 0), ("P", 0), ("U", 0), ("O", 2), ("O", 3), ("D*", 2), ("U*", 2), ("O", 4), ("O", 5),
+    ("D*", 3), ("U*", 3), ("O", 6), ("O", 7), ("D", 1), ("P", 1), ("U", 1), ("P", 2), ("V", 0), ("u", 0), ("D", 2),
+    ("P", 3), ("U", 4), ("d", 0), ("D", 3), ("U", 2), ("P", 4), ("U", 5), ("V*", 2), ("U", 3), ("D", 4), ("P", 5),
+    ("V*", 3), ("D", 5), ("P", 6), ("U", 6), ("D", 6), ("P", 7), ("U", 7), ("V", 2), ("D", 7), ("V", 1), ("d", 2),
+    ("V", 3), ("d", 1), ("u", 1), ("u", 2), ("d", 4), ("v", 0), ("d", 3), ("V", 4), ("V", 5), ("u", 3), ("d", 5),
+    ("u", 4), ("u", 6), ("V", 6), ("u", 5), ("d", 6), ("d", 7), ("u", 7), ("v", 2), ("V", 7), ("v", 3), ("v", 4),
+    ("v", 1), ("v", 6), ("v", 5), ("v", 7),
 )
 DECODE = {
-    ("O", 0): ("exchange", "project"), ("U", 1): ("rotary", "attend0"), ("V", 0): ("attend1",), ("U", 2): ("attend2",),
-    ("O", 7): ("attend3", "share"), ("P", 6): ("combine",), ("V", 7): ("finish",),
+    ("O", 0): ("start", "exchange", "project",),
+    ("O", 6): ("rotary", "attend0", "attend1",),
+    ("U", 1): ("attend2", "attend3", "share",),
+    ("V", 3): ("combine",),
+    ("u", 7): ("finish",),
 }
 F32 = jnp.float32
 BF16 = jnp.bfloat16
@@ -43,9 +47,9 @@
 def move_kernel(
     lengths, hidden, freq, old_qkv, old_out, keys, values, new_qkv, new_out,
     land, decoded,
-    packed, nq, no, hid, frq, wq, wo, kb, vb,
+    packed, early, nq, no, hid, frq, wq, wo, kb, vb,
     jown, jall, jfull, qf, ownb, part, parts, att, attf, amat,
-    lens, load_sem, recv_sem, twin_sem, send_sem, small_recv, small_send,
+    lens, load_sem, recv_sem, early_sem, twin_sem, send_sem, small_recv, small_send,
 ):
     rep = lax.axis_index("rep")
     tp = lax.axis_index("tp")
@@ -67,7 +71,8 @@
         ((new_qkv, nq), (new_out, no), (hidden, hid), (freq, frq), (old_qkv, wq), (keys, kb), (values, vb), (old_out, wo), (lengths, lens))
     ):
         c = pltpu.make_async_copy(src, dst, load_sem.at[n])
-        c.start()
+        if n < 2:
+            c.start()
         loads.append(c)
 
     barrier = pltpu.get_barrier_semaphore()
@@ -88,6 +93,8 @@
 
     loads[0].wait()
     loads[1].wait()
+    for c in loads[2:]:
+        c.start()
     for t in range(8):
         a = nq[:, QC * t : QC * (t + 1)]
         b = no[:, OC * t : OC * (t + 1)]
@@ -150,19 +157,50 @@
     def twin(slot, j):
         put(place(slot), slot, rep_of(z, x_lo, 1 - core), tp, twin_sem.at[j])
 
+    EARLY = [j for j in range(8) if ROUTE[j] == "C"]
+
+    def heir(j):
+        return ((y + 4 - ITEMS[j][0]) % 4) * 2 + x_hi
+
+    def put_early(src, j, n, r):
+        m = EARLY.index(j)
+        c = pltpu.make_async_remote_copy(
+            src_ref=src, dst_ref=early.at[m, n], send_sem=send_sem.at[1], recv_sem=early_sem.at[m, n],
+            device_id={"rep": r, "tp": tp}, device_id_type=pl.DeviceIdType.MESH,
+        )
+        c.start()
+
+    def start():
+        for j in EARLY:
+            put_early(packed.at[heir(j)], j, 0, rep_of(z_up, x_lo, core))
+            put_early(packed.at[heir(j)], j, 1, rep_of(z_dn, x_lo, core))
+
+    def handle_early(kind, j):
+        n = "DUV".index(kind)
+        block = early.at[EARLY.index(j), n]
+        all_bytes(block, early_sem.at[EARLY.index(j), n])
+        if kind == "D" and PASS_UP[j]:
+            put_early(block, j, 2, rep_of(z_up, x_lo, core))
+        if kind == "U" and not PASS_UP[j]:
+            put_early(block, j, 2, rep_of(z_dn, x_lo, core))
+        put(block, rep_of((z_dn, z_up, z_op)[n], x_lo, core) * 8 + tp, rep, heir(j))
+
     def handle(kind, j):
-        first, fwd_up = X_FIRST[j], PASS_UP[j]
+        if kind[1:]:
+            handle_early(kind[0], j)
+            return
+        first, fwd_up, along = ROUTE[j] == "A", PASS_UP[j], ROUTE[j] != "C"
         zz = {"o": z, "p": z, "d": z_dn, "u": z_up, "v": z_op}[kind.lower()]
         xx = x_lo if kind in "ODUV" else x_ot
         b = slot_of(zz, xx, ITEMS[j])
         if (kind, j) != ("O", 0):
             arrived(b)
-        if kind == "O" or (kind == "P" and first):
+        if along and (kind == "O" or (kind == "P" and first)):
             up(b)
             down(b)
-        if (kind == "D" and fwd_up) or (kind == "d" and first and not fwd_up):
+        if along and ((kind == "D" and fwd_up) or (kind == "d" and first and not fwd_up)):
             up(b)
-        if (kind == "U" and not fwd_up) or (kind == "u" and first and fwd_up):
+        if along and ((kind == "U" and not fwd_up) or (kind == "u" and first and fwd_up)):
             down(b)
         if kind == "O" or (kind in "DUV" and not first):
             across(b)
@@ -294,7 +332,7 @@
             amat[0:SEQ, :].astype(BF16), wo[...], NT, preferred_element_type=F32
         ).astype(BF16)
 
-    pieces = {"exchange": exchange, "project": project, "rotary": rotary, "share": share, "combine": combine, "finish": finish}
+    pieces = {"start": start, "exchange": exchange, "project": project, "rotary": rotary, "share": share, "combine": combine, "finish": finish}
     for event in ORDER:
         handle(*event)
         for piece in DECODE.get(event, ()):
@@ -305,6 +343,7 @@
     for j in range(8):
         all_bytes(packed, twin_sem.at[j])
     all_bytes(land.at[:, pl.ds(0, QUADS * len(sent))], send_sem.at[0])
+    all_bytes(early, send_sem.at[1])
     for phase in range(3):
         all_bytes(seven[phase], small_send.at[phase])
 
@@ -357,6 +396,7 @@
         out_specs=(vmem, vmem),
         scratch_shapes=[
             pltpu.VMEM((8, TILES, QUADS, 4, 128), BF16),
+            pltpu.VMEM((2, 3, TILES, QUADS, 4, 128), BF16),
             pltpu.VMEM((ROWS, 4608), BF16),
             pltpu.VMEM((ROWS, 3584), BF16),
             pltpu.VMEM((SEQ, 3584), BF16),
@@ -378,8 +418,9 @@
             pltpu.SMEM((SEQ,), jnp.int32),
             pltpu.SemaphoreType.DMA((9,)),
             pltpu.SemaphoreType.DMA((64,)),
+            pltpu.SemaphoreType.DMA((2, 3)),
             pltpu.SemaphoreType.DMA((8,)),
-            pltpu.SemaphoreType.DMA((1,)),
+            pltpu.SemaphoreType.DMA((2,)),
             pltpu.SemaphoreType.DMA((3,)),
             pltpu.SemaphoreType.DMA((3,)),
         ],

time: 44.1 us -> 42.2 us (0.957)
  Pallas kernels: 43.4 us -> 41.4 us
    pallas_call x1, Pallas kernels: 40 us -> 38 us  [per_device(): pl.pallas_call(move_kernel, out_shape=(pltpu.VMEM((TILES, 128 * QUADS, 4,...]
where the time goes in v6:
time: 42.2 us; the launch traced here: 42 us
  Pallas kernels  41.4 us (98%)
  between operations  0.64 us (2%)
    pallas_call x1, Pallas kernels, per_device(): pl.pallas_call(move_kernel, out_shape=(pltpu.VMEM((TILES, 128 * QUADS, 4,...  38 us
    pallas_call x1, Pallas kernels, per_device(): pl.pallas_call(write_kernel, out_shape=(pltpu.HBM((QC, 3584), BF16), pltp...  3.36 us

profile of v6, /device:TPU:1, one launch (start us, length us, event | category | flops | bytes accessed | tf_op | source)
XLA Modules:
  0.0 42.0 jit_solution(17882410389806297892)
XLA Ops:
  0.6 38.0 %move.1 = (bf16[8,896,4,128]{3,2,1,0:T(4,128)(2,1)S(1)}, bf16[4,448]{1,0:T(4,128)(2,1)S(1)}) custom-call(s32[4]{0:T(128)} %lengths.1, bf16[4,3584]{1,0:T(4,128)(2,1)} %hidden.1, f32[1,128]{1,0:T(1,128)} %constant.2.clone.freq, bf16[576,3584]{1,0:T(8,128)(2,1)} %bitcast.6, bf16[448,3584]{1,0:T(8,128)(2,1)} %bitcast.7, bf16[4,512,512]{2,1,0:T(8,128)(2,1)} %keys.1, ...), custom_call_target="tpu_custom_call" | custom-call | tf_op jit(solution)/shard_map/move/pallas_call | solution.py:392
  38.7 3.4 %write.1 = (bf16[576,3584]{1,0:T(8,128)(2,1)}, bf16[448,3584]{1,0:T(8,128)(2,1)}, bf16[4,448]{1,0:T(4,128)(2,1)}) custom-call(bf16[8,3584,128]{2,1,0:T(8,128)(2,1)S(1)} %bitcast.5, bf16[4,448]{1,0:T(4,128)(2,1)S(1)} %get-tuple-element.9.dec), custom_call_target="tpu_custom_call" | custom-call | tf_op jit(solution)/shard_map/write/pallas_call | solution.py:432

commit v7 on v6

--- a/solution.py
+++ b/solution.py
@@ -358,7 +358,7 @@
 
     d = pltpu.make_async_copy(dec, out_d, sems.at[9])
     d.start()
-    for k in range(TILES):
+    for k in (0, 1, 2, 3, 5, 6, 7, 4):
         v = land[k].T
         if k < 4:
             oq[128 * k : 128 * (k + 1)] = v

time: 42.2 us -> 42.1 us (level)
  no operation moved by 1% of the time
where the time goes in v7:
time: 42.1 us; the launch traced here: 42 us
  Pallas kernels  41.4 us (98%)
  between operations  0.64 us (2%)
    pallas_call x1, Pallas kernels, per_device(): pl.pallas_call(move_kernel, out_shape=(pltpu.VMEM((TILES, 128 * QUADS, 4,...  38 us
    pallas_call x1, Pallas kernels, per_device(): pl.pallas_call(write_kernel, out_shape=(pltpu.HBM((QC, 3584), BF16), pltp...  3.35 us

profile of v7, /device:TPU:1, one launch (start us, length us, event | category | flops | bytes accessed | tf_op | source)
XLA Modules:
  0.0 42.0 jit_solution(16486139945451015850)
XLA Ops:
  0.6 38.0 %move.1 = (bf16[8,896,4,128]{3,2,1,0:T(4,128)(2,1)S(1)}, bf16[4,448]{1,0:T(4,128)(2,1)S(1)}) custom-call(s32[4]{0:T(128)} %lengths.1, bf16[4,3584]{1,0:T(4,128)(2,1)} %hidden.1, f32[1,128]{1,0:T(1,128)} %constant.2.clone.freq, bf16[576,3584]{1,0:T(8,128)(2,1)} %bitcast.6, bf16[448,3584]{1,0:T(8,128)(2,1)} %bitcast.7, bf16[4,512,512]{2,1,0:T(8,128)(2,1)} %keys.1, ...), custom_call_target="tpu_custom_call" | custom-call | tf_op jit(solution)/shard_map/move/pallas_call | solution.py:392
  38.7 3.3 %write.1 = (bf16[576,3584]{1,0:T(8,128)(2,1)}, bf16[448,3584]{1,0:T(8,128)(2,1)}, bf16[4,448]{1,0:T(4,128)(2,1)}) custom-call(bf16[8,3584,128]{2,1,0:T(8,128)(2,1)S(1)} %bitcast.5, bf16[4,448]{1,0:T(4,128)(2,1)S(1)} %get-tuple-element.9.dec), custom_call_target="tpu_custom_call" | custom-call | tf_op jit(solution)/shard_map/write/pallas_call | solution.py:432

commit v8 on v7

--- a/solution.py
+++ b/solution.py
@@ -21,22 +21,23 @@
 PAIRS = SEQ * KVH
 
 ITEMS = ((0, 0), (0, 1), (1, 0), (3, 0), (1, 1), (3, 1), (2, 0), (2, 1))
-ROUTE = "AACCAABA"
-PASS_UP = (True, False, True, False, True, False, True, True)
+ROUTE = "ACCAAABA"
+PASS_UP = (True, True, False, False, True, False, True, True)
 ORDER = (
-    ("O", 0), ("O", 1), ("D", 0), ("P", 0), ("U", 0), ("O", 2), ("O", 3), ("D*", 2), ("U*", 2), ("O", 4), ("O", 5),
-    ("D*", 3), ("U*", 3), ("O", 6), ("O", 7), ("D", 1), ("P", 1), ("U", 1), ("P", 2), ("V", 0), ("u", 0), ("D", 2),
-    ("P", 3), ("U", 4), ("d", 0), ("D", 3), ("U", 2), ("P", 4), ("U", 5), ("V*", 2), ("U", 3), ("D", 4), ("P", 5),
-    ("V*", 3), ("D", 5), ("P", 6), ("U", 6), ("D", 6), ("P", 7), ("U", 7), ("V", 2), ("D", 7), ("V", 1), ("d", 2),
-    ("V", 3), ("d", 1), ("u", 1), ("u", 2), ("d", 4), ("v", 0), ("d", 3), ("V", 4), ("V", 5), ("u", 3), ("d", 5),
-    ("u", 4), ("u", 6), ("V", 6), ("u", 5), ("d", 6), ("d", 7), ("u", 7), ("v", 2), ("V", 7), ("v", 3), ("v", 4),
-    ("v", 1), ("v", 6), ("v", 5), ("v", 7),
+    ("O", 0), ("O", 1), ("D", 0), ("P", 0), ("U", 0), ("O", 2), ("O", 3), ("D*", 1), ("U*", 1), ("O", 4), ("O", 5),
+    ("D*", 2), ("U*", 2), ("O", 6), ("O", 7), ("P", 1), ("V", 0), ("u", 0), ("P", 2), ("D", 1), ("U", 3), ("d", 0),
+    ("P", 3), ("D", 2), ("D", 3), ("U", 1), ("U", 4), ("P", 4), ("U", 2), ("U", 5), ("V*", 1), ("P", 5), ("D", 4),
+    ("V*", 2), ("P", 6), ("D", 5), ("U", 6), ("P", 7), ("D", 6), ("U", 7), ("V", 1), ("D", 7), ("v", 0), ("d", 1),
+    ("V", 2), ("V", 3), ("d", 3), ("u", 1), ("d", 4), ("u", 3), ("d", 2), ("d", 5), ("u", 4), ("u", 2), ("V", 4),
+    ("V", 5), ("u", 6), ("d", 7), ("u", 5), ("d", 6), ("V", 6), ("u", 7), ("v", 1), ("V", 7), ("v", 4), ("v", 2),
+    ("v", 3), ("v", 5), ("v", 6), ("v", 7),
 )
 DECODE = {
     ("O", 0): ("start", "exchange", "project",),
     ("O", 6): ("rotary", "attend0", "attend1",),
-    ("U", 1): ("attend2", "attend3", "share",),
-    ("V", 3): ("combine",),
+    ("P", 1): ("attend2",),
+    ("u", 0): ("attend3", "share",),
+    ("d", 1): ("combine",),
     ("u", 7): ("finish",),
 }
 F32 = jnp.float32
@@ -160,7 +161,8 @@
     EARLY = [j for j in range(8) if ROUTE[j] == "C"]
 
     def heir(j):
-        return ((y + 4 - ITEMS[j][0]) % 4) * 2 + x_hi
+        dy, f = ITEMS[j]
+        return rep_of(z, (x_lo + f) % 2, core), ((y + 4 - dy) % 4) * 2 + (x_hi + f) % 2
 
     def put_early(src, j, n, r):
         m = EARLY.index(j)
@@ -172,8 +174,8 @@
 
     def start():
         for j in EARLY:
-            put_early(packed.at[heir(j)], j, 0, rep_of(z_up, x_lo, core))
-            put_early(packed.at[heir(j)], j, 1, rep_of(z_dn, x_lo, core))
+            put_early(packed.at[heir(j)[1]], j, 0, rep_of(z_up, x_lo, core))
+            put_early(packed.at[heir(j)[1]], j, 1, rep_of(z_dn, x_lo, core))
 
     def handle_early(kind, j):
         n = "DUV".index(kind)
@@ -183,7 +185,7 @@
             put_early(block, j, 2, rep_of(z_up, x_lo, core))
         if kind == "U" and not PASS_UP[j]:
             put_early(block, j, 2, rep_of(z_dn, x_lo, core))
-        put(block, rep_of((z_dn, z_up, z_op)[n], x_lo, core) * 8 + tp, rep, heir(j))
+        put(block, rep_of((z_dn, z_up, z_op)[n], x_lo, core) * 8 + tp, *heir(j))
 
     def handle(kind, j):
         if kind[1:]:
@@ -396,7 +398,7 @@
         out_specs=(vmem, vmem),
         scratch_shapes=[
             pltpu.VMEM((8, TILES, QUADS, 4, 128), BF16),
-            pltpu.VMEM((2, 3, TILES, QUADS, 4, 128), BF16),
+            pltpu.VMEM((ROUTE.count("C"), 3, TILES, QUADS, 4, 128), BF16),
             pltpu.VMEM((ROWS, 4608), BF16),
             pltpu.VMEM((ROWS, 3584), BF16),
             pltpu.VMEM((SEQ, 3584), BF16),
@@ -418,7 +420,7 @@
             pltpu.SMEM((SEQ,), jnp.int32),
             pltpu.SemaphoreType.DMA((9,)),
             pltpu.SemaphoreType.DMA((64,)),
-            pltpu.SemaphoreType.DMA((2, 3)),
+            pltpu.SemaphoreType.DMA((ROUTE.count("C"), 3)),
             pltpu.SemaphoreType.DMA((8,)),
             pltpu.SemaphoreType.DMA((2,)),
             pltpu.SemaphoreType.DMA((3,)),

time: 42.1 us -> 42.3 us (level)
  no operation moved by 1% of the time
where the time goes in v8:
time: 42.3 us; the launch traced here: 42.2 us
  Pallas kernels  41.6 us (98%)
  between operations  0.64 us (2%)
    pallas_call x1, Pallas kernels, per_device(): pl.pallas_call(move_kernel, out_shape=(pltpu.VMEM((TILES, 128 * QUADS, 4,...  38.2 us
    pallas_call x1, Pallas kernels, per_device(): pl.pallas_call(write_kernel, out_shape=(pltpu.HBM((QC, 3584), BF16), pltp...  3.35 us

profile of v8, /device:TPU:1, one launch (start us, length us, event | category | flops | bytes accessed | tf_op | source)
XLA Modules:
  0.0 42.2 jit_solution(14017373153846330307)
XLA Ops:
  0.6 38.2 %move.1 = (bf16[8,896,4,128]{3,2,1,0:T(4,128)(2,1)S(1)}, bf16[4,448]{1,0:T(4,128)(2,1)S(1)}) custom-call(s32[4]{0:T(128)} %lengths.1, bf16[4,3584]{1,0:T(4,128)(2,1)} %hidden.1, f32[1,128]{1,0:T(1,128)} %constant.2.clone.freq, bf16[576,3584]{1,0:T(8,128)(2,1)} %bitcast.6, bf16[448,3584]{1,0:T(8,128)(2,1)} %bitcast.7, bf16[4,512,512]{2,1,0:T(8,128)(2,1)} %keys.1, ...), custom_call_target="tpu_custom_call" | custom-call | tf_op jit(solution)/shard_map/move/pallas_call | solution.py:394
  38.8 3.3 %write.1 = (bf16[576,3584]{1,0:T(8,128)(2,1)}, bf16[448,3584]{1,0:T(8,128)(2,1)}, bf16[4,448]{1,0:T(4,128)(2,1)}) custom-call(bf16[8,3584,128]{2,1,0:T(8,128)(2,1)S(1)} %bitcast.5, bf16[4,448]{1,0:T(4,128)(2,1)S(1)} %get-tuple-element.9.dec), custom_call_target="tpu_custom_call" | custom-call | tf_op jit(solution)/shard_map/write/pallas_call | solution.py:434
